TPU v7x, 32 devices: a whole 2x2x4 slice. The times are simulated.
32 devices in a mesh: outer: 4 (over y, core), inner: 8 (over z, x).
Axes of the slice: x: 2, y: 2, z: 4, core: 2. Of those that a mesh axis runs over, the one named last changes fastest.
Arguments:
- amplitudes: float32 [2, 8388608], P(None, ('outer', 'inner')), may hold values from -200 to 200
Outputs:
- transformed: float32 [2, 8388608], P(None, ('outer', 'inner'))
- checks: float32 [3], replicated
All inputs are finite; a program needn't handle non-finite values.
Results may differ from a plain program's by a relative error of at most 0.00007.
Values sent between devices are 32-bit elements; how exact they have to be, the bound alone decides.
No kernel may reach another device: no remote copies, remote signals or barrier semaphores. Data moves between devices by JAX's collectives and lax.ppermute only.
A program may use at most 64 MiB of HBM per device.

v0:
```python
import math

import jax
import jax.numpy as jnp
import ml_dtypes
import numpy as np
from jax import lax
from jax.experimental import pallas as pl
from jax.experimental.pallas import tpu as pltpu
from jax.sharding import PartitionSpec as P

WINDOW = 9
LANES = 128
RADIX = 2**WINDOW // LANES
AXES = ("outer", "inner")


def flip(value, count):
    result = 0
    for bit_pos in range(count):
        result |= (value >> bit_pos & 1) << count - 1 - bit_pos
    return result


def split_halves(table):
    high = table.astype(ml_dtypes.bfloat16)
    low = (table - high.astype(np.float64)).astype(ml_dtypes.bfloat16)
    return high, low


def transform_tables():
    columns = 2**WINDOW
    freq = np.arange(LANES) * RADIX
    sample = np.arange(LANES)
    tables = []
    for residue in range(RADIX):
        angles = (freq + residue)[:, None] * sample[None, :] % columns * (2 * np.pi / columns)
        cosine = np.cos(angles) / math.sqrt(columns)
        sine = np.sin(angles) / math.sqrt(columns)
        rows = np.stack([np.concatenate([cosine, -sine], 1), np.concatenate([sine, cosine], 1)], 1)
        tables.append(rows.reshape(2 * LANES, 2 * LANES))
    return split_halves(np.stack(tables))


def halves(values):
    high = values.astype(jnp.bfloat16)
    low = (values - high.astype(jnp.float32)).astype(jnp.bfloat16)
    return high, low


def dot_rows(left, right):
    return lax.dot_general(
        left, right, (((1,), (1,)), ((), ())), preferred_element_type=jnp.float32
    )


def transform_kernel(
    info, x_ref, high_ref, low_ref, order_ref, send_ref, stage, square_sum, real_sum, imag_sum, sems
):
    n_devices, chunks, angle_scale, device_id = info()
    chunk = pl.program_id(0)
    chunk_rows = RADIX * 8

    @pl.when(chunk == 0)
    def _():
        square_sum[...] = jnp.zeros_like(square_sum)
        real_sum[...] = jnp.zeros_like(real_sum)
        imag_sum[...] = jnp.zeros_like(imag_sum)

    parts = [
        [x_ref[pl.ds(2 * j + s, LANES, stride=2 * RADIX), :] for s in range(2)]
        for j in range(RADIX)
    ]
    squares = sum(p * p for pair in parts for p in pair)
    square_sum[...] += squares.reshape(LANES // 8, 8, LANES).sum(0)

    dev_bits = n_devices.bit_length() - 1
    chunk_bits = chunks.bit_length() - 1
    base = jnp.int32(0)
    for bit in range(dev_bits):
        base += (device_id >> bit & 1) << (dev_bits - 1 - bit)
    for bit in range(chunk_bits):
        base += (chunk >> bit & 1) << (dev_bits + chunk_bits - 1 - bit)
    theta = (order_ref[...] * float(n_devices * chunks) + base.astype(jnp.float32)) * angle_scale
    lane = lax.broadcasted_iota(jnp.int32, (LANES, LANES), 1)
    theta_sq = theta * theta
    cosine = 1.0 - theta_sq * (0.5 - theta_sq * (1.0 / 24.0))
    sine = theta * (1.0 - theta_sq * (1.0 / 6.0 - theta_sq * (1.0 / 120.0)))
    cosine = jnp.where(lane == 1, cosine, 0.0)
    sine = jnp.where(lane == 1, sine, 0.0)
    first_re, first_im = parts[0]
    real_terms = first_re * cosine + first_im * sine
    imag_terms = first_im * cosine - first_re * sine
    real_sum[...] += real_terms.reshape(LANES // 8, 8, LANES).sum(0)
    imag_sum[...] += imag_terms.reshape(LANES // 8, 8, LANES).sum(0)

    (r0, i0), (r1, i1), (r2, i2), (r3, i3) = parts
    ar, ai, br, bi = r0 + r2, i0 + i2, r0 - r2, i0 - i2
    cr, ci, dr, di = r1 + r3, i1 + i3, r1 - r3, i1 - i3
    folded = [(ar + cr, ai + ci), (br - di, bi + dr), (ar - cr, ai - ci), (br + di, bi - dr)]
    for residue in range(RADIX):
        high, low = halves(jnp.concatenate(folded[residue], 1))
        table = high_ref[residue]
        values = dot_rows(table, high) + dot_rows(table, low) + dot_rows(low_ref[residue], high)
        row = pl.multiple_of(chunk * chunk_rows + residue * 8, 8)
        stage[:, pl.ds(row, 8), :] = values.reshape(n_devices, 8, LANES)

    def send(step):
        rows = pl.ds(pl.multiple_of(step * chunk_rows, 8), chunk_rows)
        return pltpu.make_async_copy(stage.at[:, rows], send_ref.at[:, rows], sems.at[step])

    send(chunk).start()

    @pl.when(chunk == chunks - 1)
    def _():
        rows = pl.ds(chunks * chunk_rows, 8)
        sums = [ref[...].sum(0, keepdims=True) for ref in (square_sum, real_sum, imag_sum)]
        tile = jnp.concatenate(sums + [jnp.zeros((5, LANES), jnp.float32)], 0)
        stage[:, rows, :] = jnp.broadcast_to(tile[None], (n_devices, 8, LANES))
        last = pltpu.make_async_copy(stage.at[:, rows], send_ref.at[:, rows], sems.at[chunks])
        last.start()
        for step in range(chunks):
            send(step).wait()
        last.wait()


def place_kernel(info, recv_ref, order_ref, out_ref, checks_ref, held, factor_ref, sems):
    n_devices, chunks, total_len = info
    group = pl.program_id(0)
    dev_bits = n_devices.bit_length() - 1
    chunk_bits = chunks.bit_length() - 1
    slot_rows = held.shape[0] // n_devices

    @pl.when(group == 0)
    def _():
        copies = [
            pltpu.make_async_copy(
                recv_ref.at[source],
                held.at[pl.ds(flip(source, dev_bits) * slot_rows, slot_rows)],
                sems.at[source],
            )
            for source in range(n_devices)
        ]
        for copy in copies:
            copy.start()
        for copy in copies:
            copy.wait()
        tile = held[pl.ds(slot_rows - 8, 8), :]
        for source in range(1, n_devices):
            tile = tile + held[pl.ds(source * slot_rows + slot_rows - 8, 8), :]
        sums = tile.sum(1, keepdims=True)
        mean_square = jnp.broadcast_to(sums[0:1], (8, LANES)) * (1.0 / total_len)
        shifted = mean_square + 1e-06
        factor = lax.rsqrt(shifted)
        factor = factor * (1.5 - 0.5 * shifted * factor * factor)
        factor_ref[...] = factor
        columns = 2**WINDOW
        scaled = factor * math.sqrt(columns / total_len)
        checks_ref[0] = mean_square[0, 0]
        checks_ref[1] = (jnp.broadcast_to(sums[1:2], (8, LANES)) * scaled)[0, 0]
        checks_ref[2] = (jnp.broadcast_to(sums[2:3], (8, LANES)) * scaled)[0, 0]

    factor = jnp.broadcast_to(factor_ref[0:1], (LANES, LANES))
    order = order_ref[...]
    for residue in range(RADIX):
        for part in range(2):
            pieces = []
            for low in range(chunks):
                tile_row = (flip(low, chunk_bits) * RADIX + residue) * 8 + part
                pieces.append(held[pl.ds(tile_row + 2 * group, n_devices, stride=slot_rows), :])
            high, low = halves(jnp.concatenate(pieces, 0))
            turned = dot_rows(order, jnp.concatenate([high, low], 1))
            out_ref[pl.ds(residue * 2 * LANES + part, LANES, stride=2), :] = turned * factor


def reverse_index(values, count):
    result = jnp.zeros_like(values)
    for bit_pos in range(count):
        result = result | (values >> bit_pos & 1) << count - 1 - bit_pos
    return result


def reversal_table(size, count):
    indices = jnp.arange(size, dtype=jnp.int32)
    return (reverse_index(indices, count)[:, None] == indices[None, :]).astype(jnp.float32)


def check_terms(current, positions, angle_scale):
    angles = positions.astype(jnp.float32) * angle_scale
    cosine = jnp.cos(angles)
    sine = jnp.sin(angles)
    squares = jnp.sum(current * current)
    phase_real = jnp.sum(current[0] * cosine + current[1] * sine)
    phase_imag = jnp.sum(current[1] * cosine - current[0] * sine)
    return (squares, phase_real, phase_imag)


def general_device(amplitudes):
    amp_dev = amplitudes.shape[1]
    n_outer = lax.axis_size("outer")
    n_inner = lax.axis_size("inner")
    outer_bits = n_outer.bit_length() - 1
    inner_bits = n_inner.bit_length() - 1
    global_bits = outer_bits + inner_bits
    local_bits = amp_dev.bit_length() - 1
    n_devices = n_outer * n_inner
    high_count = amp_dev // n_devices
    total_len = amp_dev * n_devices
    columns = 2**WINDOW
    rows_count = amp_dev // columns
    column_ids = jnp.arange(columns, dtype=jnp.int32)
    reversed_ids = reverse_index(column_ids, WINDOW)
    products = column_ids[:, None] * reversed_ids[None, :] % columns
    angles = products.astype(jnp.float32) * (2.0 * math.pi / columns)
    real_part = jnp.cos(angles) / math.sqrt(columns)
    imag_part = jnp.sin(angles) / math.sqrt(columns)
    table = jnp.concatenate(
        [jnp.concatenate([real_part, imag_part], 1), jnp.concatenate([-imag_part, real_part], 1)], 0
    )
    stacked = jnp.concatenate(
        [amplitudes[0].reshape(rows_count, columns), amplitudes[1].reshape(rows_count, columns)], 1
    )
    result = jnp.dot(
        stacked, table, precision=lax.Precision.HIGHEST, preferred_element_type=jnp.float32
    )
    windowed = jnp.stack([result[:, :columns].reshape(-1), result[:, columns:].reshape(-1)])
    device_id = lax.axis_index("outer") * n_inner + lax.axis_index("inner")
    angle_scale = 2.0 * math.pi / total_len
    local_ids = jnp.arange(amp_dev, dtype=jnp.int32)
    positions = reverse_index(device_id * amp_dev + local_ids, local_bits + global_bits)
    totals = lax.psum(check_terms(windowed, positions, angle_scale), ("outer", "inner"))
    device_table = reversal_table(n_devices, global_bits)
    high_table = reversal_table(high_count, local_bits - global_bits)
    grid = windowed.reshape(2, high_count, n_devices)
    ordered = jnp.einsum("pm,shm->sph", device_table, grid, precision=lax.Precision.HIGHEST)
    blocks = ordered.reshape(2, n_outer, n_inner, high_count)
    blocks = lax.all_to_all(
        lax.all_to_all(blocks, "outer", split_axis=1, concat_axis=1, tiled=True),
        "inner",
        split_axis=2,
        concat_axis=2,
        tiled=True,
    )
    received = blocks.reshape(2, n_devices, high_count)
    turned_high = jnp.einsum("qh,sdh->sdq", high_table, received, precision=lax.Precision.HIGHEST)
    placed = jnp.einsum("ed,sdq->sqe", device_table, turned_high, precision=lax.Precision.HIGHEST)
    reversed_field = placed.reshape(2, amp_dev)
    mean_square = totals[0] / total_len
    factor = lax.rsqrt(mean_square + 1e-06)
    scaled = factor / math.sqrt(total_len)
    checks = jnp.stack([mean_square, totals[1] * scaled, totals[2] * scaled])
    return (reversed_field * factor, checks)


def per_device(amplitudes):
    amp_dev = amplitudes.shape[1]
    n_devices = lax.axis_size("outer") * lax.axis_size("inner")
    n_inner = lax.axis_size("inner")
    total_len = amp_dev * n_devices
    columns = 2**WINDOW
    rows_count = amp_dev // columns
    chunks = rows_count // LANES
    groups = columns // n_devices // RADIX
    if chunks * n_devices != LANES or groups * 2 != 8:
        return general_device(amplitudes)
    vectors = 2 * amp_dev // LANES
    slot_rows = chunks * RADIX * 8 + 8
    x = amplitudes.reshape(2, vectors // 2, LANES).transpose(1, 0, 2).reshape(vectors, LANES)
    high, low = transform_tables()
    turn = np.array([flip(lane, LANES.bit_length() - 1) for lane in range(LANES)])
    order = (turn[:, None] == np.arange(LANES)[None, :]).astype(np.float32)
    order = np.concatenate([order, order], 1).astype(ml_dtypes.bfloat16)
    turn_table = np.broadcast_to(turn[:, None], (LANES, LANES)).astype(np.float32)

    def info():
        device_id = lax.axis_index("outer") * n_inner + lax.axis_index("inner")
        return n_devices, chunks, 2.0 * math.pi / total_len, device_id

    whole = lambda shape: pl.BlockSpec(shape, lambda i: (0,) * len(shape))
    sent = pl.pallas_call(
        lambda *refs: transform_kernel(info, *refs),
        grid=(chunks,),
        in_specs=[
            pl.BlockSpec((vectors // chunks, LANES), lambda i: (i, 0)),
            whole(high.shape),
            whole(low.shape),
            whole(turn_table.shape),
        ],
        out_specs=pl.BlockSpec(memory_space=pltpu.HBM),
        out_shape=jax.ShapeDtypeStruct((n_devices, slot_rows, LANES), jnp.float32),
        scratch_shapes=[
            pltpu.VMEM((n_devices, slot_rows, LANES), jnp.float32),
            pltpu.VMEM((8, LANES), jnp.float32),
            pltpu.VMEM((8, LANES), jnp.float32),
            pltpu.VMEM((8, LANES), jnp.float32),
            pltpu.SemaphoreType.DMA((chunks + 1,)),
        ],
        name="transform",
    )(x, jnp.asarray(high), jnp.asarray(low), jnp.asarray(turn_table))
    received = lax.all_to_all(sent, AXES, 0, 0, tiled=True)
    placed, checks = pl.pallas_call(
        lambda *refs: place_kernel((n_devices, chunks, total_len), *refs),
        grid=(groups,),
        in_specs=[pl.BlockSpec(memory_space=pltpu.HBM), whole(order.shape)],
        out_specs=[
            pl.BlockSpec((vectors // groups, LANES), lambda i: (i, 0)),
            pl.BlockSpec(memory_space=pltpu.SMEM),
        ],
        out_shape=[
            jax.ShapeDtypeStruct((vectors, LANES), jnp.float32),
            jax.ShapeDtypeStruct((3,), jnp.float32),
        ],
        scratch_shapes=[
            pltpu.VMEM((n_devices * slot_rows, LANES), jnp.float32),
            pltpu.VMEM((8, LANES), jnp.float32),
            pltpu.SemaphoreType.DMA((n_devices,)),
        ],
        name="place",
    )(received, jnp.asarray(order))
    placed = placed.reshape(vectors // 2, 2, LANES).transpose(1, 0, 2).reshape(2, amp_dev)
    return placed, checks


def solution(mesh):
    return jax.shard_map(
        per_device,
        mesh=mesh,
        in_specs=(P(None, ("outer", "inner")),),
        out_specs=(P(None, ("outer", "inner")), P()),
        check_vma=False,
    )
```

profile of v0, /device:TPU:0, one launch (start us, length us, event | category | flops | bytes accessed | tf_op | source)
XLA Modules:
  0.0 72.0 jit_solution(12521313929059248863)
XLA Ops:
  0.6 5.7 %transform.1 = f32[32,136,128]{2,1,0:T(8,128)} custom-call(f32[4096,128]{1,0:T(8,128)} %bitcast.10, bf16[4,256,256]{2,1,0:T(8,128)(2,1)} %constant.8.clone.refs_1_, bf16[4,256,256]{2,1,0:T(8,128)(2,1)} %constant.9.clone.refs_2_, f32[128,128]{1,0:T(8,128)} %constant.10.clone.refs_3_), custom_call_target="tpu_custom_call" | custom-call | tf_op jit(solution)/shard_map/transform/pallas_call | solution.py:280
  6.3 60.2 %all_to_all.5.refs_0_ = f32[32,136,128]{2,1,0:T(8,128)} all-to-all(f32[32,136,128]{2,1,0:T(8,128)} %transform.1), channel_id=1, replica_groups=mesh['outer'=4,'inner'=8] {'outer','inner'}, dimensions={0} | all-to-all | bytes 4456448 | tf_op jit(solution)/shard_map/all_to_all | solution.py:300
  66.5 5.5 %place.1 = (f32[4096,128]{1,0:T(8,128)}, f32[3]{0:T(128)}) custom-call(f32[32,136,128]{2,1,0:T(8,128)} %all_to_all.5.refs_0_, bf16[128,256]{1,0:T(8,128)(2,1)} %constant.11.clone.refs_1_), custom_call_target="tpu_custom_call" | custom-call | tf_op jit(solution)/shard_map/place/pallas_call | solution.py:301
where the time goes:
time: 72.4 us; the launch traced here: 72 us
  blocking collectives  60.2 us (83%)
  Pallas kernels  11.2 us (15%)
    all_to_all x1, blocking collectives, per_device(): received = lax.all_to_all(sent, AXES, 0, 0, tiled=True)  60.2 us
    pallas_call x1, Pallas kernels, per_device(): pl.pallas_call(lambda *refs: transform_kernel(info, *refs), grid=(chunks,...  5.7 us
    pallas_call x1, Pallas kernels, per_device(): pl.pallas_call(lambda *refs: place_kernel((n_devices, chunks, total_len),...  5.48 us

commit v1 on v0

--- a/solution.py
+++ b/solution.py
@@ -9,10 +9,12 @@
 from jax.experimental.pallas import tpu as pltpu
 from jax.sharding import PartitionSpec as P
 
+
 WINDOW = 9
 LANES = 128
 RADIX = 2**WINDOW // LANES
 AXES = ("outer", "inner")
+VMEM_LIMIT = 16 * 2**20
 
 
 def flip(value, count):
@@ -54,78 +56,101 @@
     )
 
 
-def transform_kernel(
-    info, x_ref, high_ref, low_ref, order_ref, send_ref, stage, square_sum, real_sum, imag_sum, sems
-):
+def transform_kernel(info, targets, tiles, x_hbm, high_hbm, low_hbm, order_hbm, *refs):
     n_devices, chunks, angle_scale, device_id = info()
-    chunk = pl.program_id(0)
+    outs, (x_ref, high_ref, low_ref, order_ref, stage, sems) = refs[:-6], refs[-6:]
     chunk_rows = RADIX * 8
-
-    @pl.when(chunk == 0)
-    def _():
-        square_sum[...] = jnp.zeros_like(square_sum)
-        real_sum[...] = jnp.zeros_like(real_sum)
-        imag_sum[...] = jnp.zeros_like(imag_sum)
-
-    parts = [
-        [x_ref[pl.ds(2 * j + s, LANES, stride=2 * RADIX), :] for s in range(2)]
-        for j in range(RADIX)
-    ]
-    squares = sum(p * p for pair in parts for p in pair)
-    square_sum[...] += squares.reshape(LANES // 8, 8, LANES).sum(0)
-
+    x_rows = x_ref.shape[0] // chunks
     dev_bits = n_devices.bit_length() - 1
     chunk_bits = chunks.bit_length() - 1
+
+    def load(source, target, index):
+        return pltpu.make_async_copy(source, target, sems.at[index])
+
+    loads = []
+    for chunk in range(chunks):
+        rows = pl.ds(chunk * x_rows, x_rows)
+        loads.append(load(x_hbm.at[rows], x_ref.at[rows], chunk))
+    sides = [load(order_hbm, order_ref, chunks)]
+    tables = []
+    for residue in range(RADIX):
+        index = chunks + 1 + 2 * residue
+        tables.append(
+            [
+                load(high_hbm.at[residue], high_ref.at[residue], index),
+                load(low_hbm.at[residue], low_ref.at[residue], index + 1),
+            ]
+        )
+    for copy in loads[:1] + sides + sum(tables, []) + loads[1:]:
+        copy.start()
+
     base = jnp.int32(0)
     for bit in range(dev_bits):
         base += (device_id >> bit & 1) << (dev_bits - 1 - bit)
-    for bit in range(chunk_bits):
-        base += (chunk >> bit & 1) << (dev_bits + chunk_bits - 1 - bit)
-    theta = (order_ref[...] * float(n_devices * chunks) + base.astype(jnp.float32)) * angle_scale
     lane = lax.broadcasted_iota(jnp.int32, (LANES, LANES), 1)
-    theta_sq = theta * theta
-    cosine = 1.0 - theta_sq * (0.5 - theta_sq * (1.0 / 24.0))
-    sine = theta * (1.0 - theta_sq * (1.0 / 6.0 - theta_sq * (1.0 / 120.0)))
-    cosine = jnp.where(lane == 1, cosine, 0.0)
-    sine = jnp.where(lane == 1, sine, 0.0)
-    first_re, first_im = parts[0]
-    real_terms = first_re * cosine + first_im * sine
-    imag_terms = first_im * cosine - first_re * sine
-    real_sum[...] += real_terms.reshape(LANES // 8, 8, LANES).sum(0)
-    imag_sum[...] += imag_terms.reshape(LANES // 8, 8, LANES).sum(0)
-
-    (r0, i0), (r1, i1), (r2, i2), (r3, i3) = parts
-    ar, ai, br, bi = r0 + r2, i0 + i2, r0 - r2, i0 - i2
-    cr, ci, dr, di = r1 + r3, i1 + i3, r1 - r3, i1 - i3
-    folded = [(ar + cr, ai + ci), (br - di, bi + dr), (ar - cr, ai - ci), (br + di, bi - dr)]
-    for residue in range(RADIX):
-        high, low = halves(jnp.concatenate(folded[residue], 1))
-        table = high_ref[residue]
-        values = dot_rows(table, high) + dot_rows(table, low) + dot_rows(low_ref[residue], high)
-        row = pl.multiple_of(chunk * chunk_rows + residue * 8, 8)
-        stage[:, pl.ds(row, 8), :] = values.reshape(n_devices, 8, LANES)
-
-    def send(step):
-        rows = pl.ds(pl.multiple_of(step * chunk_rows, 8), chunk_rows)
-        return pltpu.make_async_copy(stage.at[:, rows], send_ref.at[:, rows], sems.at[step])
-
-    send(chunk).start()
-
-    @pl.when(chunk == chunks - 1)
-    def _():
-        rows = pl.ds(chunks * chunk_rows, 8)
-        sums = [ref[...].sum(0, keepdims=True) for ref in (square_sum, real_sum, imag_sum)]
-        tile = jnp.concatenate(sums + [jnp.zeros((5, LANES), jnp.float32)], 0)
-        stage[:, rows, :] = jnp.broadcast_to(tile[None], (n_devices, 8, LANES))
-        last = pltpu.make_async_copy(stage.at[:, rows], send_ref.at[:, rows], sems.at[chunks])
-        last.start()
-        for step in range(chunks):
-            send(step).wait()
-        last.wait()
-
-
-def place_kernel(info, recv_ref, order_ref, out_ref, checks_ref, held, factor_ref, sems):
-    n_devices, chunks, total_len = info
+    square_sum = real_sum = imag_sum = jnp.zeros((8, LANES), jnp.float32)
+    for chunk in range(chunks):
+        loads[chunk].wait()
+        parts = [
+            [
+                x_ref[pl.ds(chunk * x_rows + 2 * j + s, LANES, stride=2 * RADIX), :]
+                for s in range(2)
+            ]
+            for j in range(RADIX)
+        ]
+        squares = sum(p * p for pair in parts for p in pair)
+        square_sum += squares.reshape(LANES // 8, 8, LANES).sum(0)
+
+        if chunk == 0:
+            sides[0].wait()
+        offset = (base + n_devices * flip(chunk, chunk_bits)).astype(jnp.float32)
+        theta = (order_ref[...] * float(n_devices * chunks) + offset) * angle_scale
+        theta_sq = theta * theta
+        cosine = 1.0 - theta_sq * (0.5 - theta_sq * (1.0 / 24.0))
+        sine = theta * (1.0 - theta_sq * (1.0 / 6.0 - theta_sq * (1.0 / 120.0)))
+        cosine = jnp.where(lane == 1, cosine, 0.0)
+        sine = jnp.where(lane == 1, sine, 0.0)
+        first_re, first_im = parts[0]
+        real_terms = first_re * cosine + first_im * sine
+        imag_terms = first_im * cosine - first_re * sine
+        real_sum += real_terms.reshape(LANES // 8, 8, LANES).sum(0)
+        imag_sum += imag_terms.reshape(LANES // 8, 8, LANES).sum(0)
+
+        (r0, i0), (r1, i1), (r2, i2), (r3, i3) = parts
+        ar, ai, br, bi = r0 + r2, i0 + i2, r0 - r2, i0 - i2
+        cr, ci, dr, di = r1 + r3, i1 + i3, r1 - r3, i1 - i3
+        folded = [(ar + cr, ai + ci), (br - di, bi + dr), (ar - cr, ai - ci), (br + di, bi - dr)]
+        for residue in range(RADIX):
+            high, low = halves(jnp.concatenate(folded[residue], 1))
+            if chunk == 0:
+                for copy in tables[residue]:
+                    copy.wait()
+            table = high_ref[residue]
+            values = dot_rows(table, high) + dot_rows(table, low) + dot_rows(low_ref[residue], high)
+            stage[:, residue * 8 : residue * 8 + 8, :] = values.reshape(n_devices, 8, LANES)
+        for mask, out, row in targets:
+            rows = pl.ds(row + chunk * chunk_rows, chunk_rows)
+            outs[out][rows, :] = stage[device_id ^ mask]
+
+    sums = [value.sum(0, keepdims=True) for value in (square_sum, real_sum, imag_sum)]
+    tile = jnp.concatenate(sums + [jnp.zeros((5, LANES), jnp.float32)], 0)
+    for out, row in tiles:
+        outs[out][pl.ds(row, 8), :] = tile
+
+
+def join_kernel(plan, n_join, swapped_ref, own_ref, *refs):
+    outs = refs[n_join:]
+    rows, tile_row = plan
+    tile = swapped_ref[pl.ds(tile_row, 8), :] + own_ref[pl.ds(rows, 8), :]
+    for index in range(n_join):
+        outs[index][pl.ds(rows, rows), :] = swapped_ref[pl.ds(index * rows, rows), :]
+        outs[index][pl.ds(2 * rows, 8), :] = tile
+
+
+def place_kernel(info, sources, tiles, order_ref, *refs):
+    n_devices, chunks, total_len, device_id = info()
+    ins = refs[:-4]
+    out_ref, checks_ref, held, factor_ref = refs[-4:]
     group = pl.program_id(0)
     dev_bits = n_devices.bit_length() - 1
     chunk_bits = chunks.bit_length() - 1
@@ -133,21 +158,17 @@
 
     @pl.when(group == 0)
     def _():
-        copies = [
-            pltpu.make_async_copy(
-                recv_ref.at[source],
-                held.at[pl.ds(flip(source, dev_bits) * slot_rows, slot_rows)],
-                sems.at[source],
-            )
-            for source in range(n_devices)
-        ]
-        for copy in copies:
-            copy.start()
-        for copy in copies:
-            copy.wait()
-        tile = held[pl.ds(slot_rows - 8, 8), :]
-        for source in range(1, n_devices):
-            tile = tile + held[pl.ds(source * slot_rows + slot_rows - 8, 8), :]
+        turned_id = jnp.int32(0)
+        for bit in range(dev_bits):
+            turned_id += (device_id >> bit & 1) << (dev_bits - 1 - bit)
+        rows = chunks * RADIX * 8
+        for mask, array, offset in sources:
+            slot = turned_id ^ flip(mask, dev_bits)
+            target = pl.ds(pl.multiple_of(slot * slot_rows, 8), rows)
+            held[target, :] = ins[array][pl.ds(offset, rows), :]
+        tile = jnp.zeros((8, LANES), jnp.float32)
+        for array, offset in tiles:
+            tile = tile + ins[array][pl.ds(offset, 8), :]
         sums = tile.sum(1, keepdims=True)
         mean_square = jnp.broadcast_to(sums[0:1], (8, LANES)) * (1.0 / total_len)
         shifted = mean_square + 1e-06
@@ -272,36 +293,83 @@
     order = np.concatenate([order, order], 1).astype(ml_dtypes.bfloat16)
     turn_table = np.broadcast_to(turn[:, None], (LANES, LANES)).astype(np.float32)
 
+    rows = chunks * RADIX * 8
+    core_bit = n_inner
+    far_bit = n_inner // 2
+    weight = lambda mask: mask.bit_count()
+    chip_masks = [mask for mask in range(n_devices) if not mask & core_bit]
+    far = sorted([mask for mask in chip_masks if mask & far_bit], key=weight)
+    near = sorted([mask for mask in chip_masks if mask and not mask & far_bit], key=weight)
+    direct, pairs = far[:2], far[2:] + near
+    n_pairs = len(pairs)
+
     def info():
         device_id = lax.axis_index("outer") * n_inner + lax.axis_index("inner")
         return n_devices, chunks, 2.0 * math.pi / total_len, device_id
 
+    def place_info():
+        return n_devices, chunks, total_len, info()[3]
+
+    def exchange(values, mask):
+        pairs_of = [(source, source ^ mask) for source in range(n_devices)]
+        return lax.ppermute(values, AXES, pairs_of)
+
+    singles = [mask ^ core for mask in direct for core in (0, core_bit)]
+    swap_rows = (n_pairs + 1) * rows
+    shapes = [(2 * rows + 8, LANES)] * n_pairs + [(rows + 8, LANES), (swap_rows + 8, LANES)]
+    shapes += [(rows + 8, LANES)] * len(singles)
+    stay, swap = n_pairs, n_pairs + 1
+    targets = [(mask, index, 0) for index, mask in enumerate(pairs)] + [(0, stay, 0)]
+    targets += [(mask ^ core_bit, swap, index * rows) for index, mask in enumerate(pairs + [0])]
+    targets += [(mask, swap + 1 + index, 0) for index, mask in enumerate(singles)]
+    tiles = [(stay, rows), (swap, swap_rows)]
+    tiles += [(swap + 1 + index, rows) for index in range(len(singles))]
     whole = lambda shape: pl.BlockSpec(shape, lambda i: (0,) * len(shape))
+    hbm = pl.BlockSpec(memory_space=pltpu.HBM)
+    vmem = pl.BlockSpec(memory_space=pltpu.VMEM)
     sent = pl.pallas_call(
-        lambda *refs: transform_kernel(info, *refs),
-        grid=(chunks,),
-        in_specs=[
-            pl.BlockSpec((vectors // chunks, LANES), lambda i: (i, 0)),
-            whole(high.shape),
-            whole(low.shape),
-            whole(turn_table.shape),
+        lambda *refs: transform_kernel(info, targets, tiles, *refs),
+        in_specs=[hbm] * 4,
+        out_specs=[vmem] * len(shapes),
+        out_shape=[jax.ShapeDtypeStruct(shape, jnp.float32) for shape in shapes],
+        scratch_shapes=[
+            pltpu.VMEM((vectors, LANES), jnp.float32),
+            pltpu.VMEM(high.shape, jnp.bfloat16),
+            pltpu.VMEM(low.shape, jnp.bfloat16),
+            pltpu.VMEM(turn_table.shape, jnp.float32),
+            pltpu.VMEM((n_devices, RADIX * 8, LANES), jnp.float32),
+            pltpu.SemaphoreType.DMA((chunks + 1 + 2 * RADIX,)),
         ],
-        out_specs=pl.BlockSpec(memory_space=pltpu.HBM),
-        out_shape=jax.ShapeDtypeStruct((n_devices, slot_rows, LANES), jnp.float32),
-        scratch_shapes=[
-            pltpu.VMEM((n_devices, slot_rows, LANES), jnp.float32),
-            pltpu.VMEM((8, LANES), jnp.float32),
-            pltpu.VMEM((8, LANES), jnp.float32),
-            pltpu.VMEM((8, LANES), jnp.float32),
-            pltpu.SemaphoreType.DMA((chunks + 1,)),
-        ],
+        compiler_params=pltpu.CompilerParams(vmem_limit_bytes=VMEM_LIMIT),
         name="transform",
-    )(x, jnp.asarray(high), jnp.asarray(low), jnp.asarray(turn_table))
-    received = lax.all_to_all(sent, AXES, 0, 0, tiled=True)
+    )(*[pltpu.with_memory_space_constraint(a, pltpu.HBM) for a in (x, jnp.asarray(high), jnp.asarray(low), jnp.asarray(turn_table))])
+    swapped = exchange(sent[swap], core_bit)
+    arrived_singles = []
+    for index, mask in enumerate(singles):
+        arrived_singles.append(exchange(sent[swap + 1 + index], mask))
+    joined = pl.pallas_call(
+        lambda *refs: join_kernel((rows, swap_rows), n_pairs, *refs),
+        in_specs=[vmem] * (2 + n_pairs),
+        out_specs=[vmem] * n_pairs,
+        out_shape=[jax.ShapeDtypeStruct(shapes[0], jnp.float32)] * n_pairs,
+        input_output_aliases={2 + i: i for i in range(n_pairs)},
+        compiler_params=pltpu.CompilerParams(vmem_limit_bytes=VMEM_LIMIT),
+        name="join",
+    )(swapped, sent[stay], *sent[:n_pairs])
+    arrived_pairs = []
+    for index, mask in enumerate(pairs):
+        arrived_pairs.append(exchange(joined[index], mask))
+    arrivals = arrived_pairs + [sent[stay], swapped] + arrived_singles
+    sources = []
+    for index, mask in enumerate(pairs):
+        sources += [(mask, index, 0), (mask ^ core_bit, index, rows)]
+    sources += [(0, stay, 0), (core_bit, swap, n_pairs * rows)]
+    sources += [(mask, swap + 1 + index, 0) for index, mask in enumerate(singles)]
+    tiles = [(index, 2 * rows) for index in range(n_pairs)] + tiles
     placed, checks = pl.pallas_call(
-        lambda *refs: place_kernel((n_devices, chunks, total_len), *refs),
+        lambda *refs: place_kernel(place_info, sources, tiles, *refs),
         grid=(groups,),
-        in_specs=[pl.BlockSpec(memory_space=pltpu.HBM), whole(order.shape)],
+        in_specs=[whole(order.shape)] + [vmem] * len(arrivals),
         out_specs=[
             pl.BlockSpec((vectors // groups, LANES), lambda i: (i, 0)),
             pl.BlockSpec(memory_space=pltpu.SMEM),
@@ -313,10 +381,10 @@
         scratch_shapes=[
             pltpu.VMEM((n_devices * slot_rows, LANES), jnp.float32),
             pltpu.VMEM((8, LANES), jnp.float32),
-            pltpu.SemaphoreType.DMA((n_devices,)),
         ],
+        compiler_params=pltpu.CompilerParams(vmem_limit_bytes=VMEM_LIMIT),
         name="place",
-    )(received, jnp.asarray(order))
+    )(jnp.asarray(order), *arrivals)
     placed = placed.reshape(vectors // 2, 2, LANES).transpose(1, 0, 2).reshape(2, amp_dev)
     return placed, checks
 

time: 72.4 us -> 77.9 us (1.076)
  blocking collectives: 60.2 us -> 0 us
  waiting for transfers between devices: 0 us -> 34.6 us
  starting transfers between devices: 0 us -> 34.5 us
  Pallas kernels: 11.2 us -> 7.99 us
    all_to_all x1 -> x0, blocking collectives: 60.2 us -> none  [per_device(): received = lax.all_to_all(sent, AXES, 0, 0, tiled=True)]
    ppermute x0 -> x18, waiting for transfers between devices: none -> 34.6 us  [exchange(): return lax.ppermute(values, AXES, pairs_of)]
    ppermute x0 -> x18, starting transfers between devices: none -> 34.5 us  [exchange(): return lax.ppermute(values, AXES, pairs_of)]
    pallas_call x2 -> x3, Pallas kernels: 11.2 us -> 7.99 us  [the longest x1 5.07 us: per_device(): pl.pallas_call(lambda *refs: transform_kernel(info, targets, tiles, *refs...]
  transfers between devices with their start and end apart: 0 -> 18, of which waited for: 0 -> 7; matrix products, arithmetic and copies ran while one was open for 0% -> 0% of each run, Pallas kernels for 0% -> 0%
where the time goes in v1:
time: 77.9 us; the launch traced here: 77.7 us
  waiting for transfers between devices  34.6 us (44%)
  starting transfers between devices  34.5 us (44%)
  Pallas kernels  7.99 us (10%)
    ppermute x18, waiting for transfers between devices, exchange(): return lax.ppermute(values, AXES, pairs_of)  34.6 us
    ppermute x18, starting transfers between devices, exchange(): return lax.ppermute(values, AXES, pairs_of)  34.5 us
    pallas_call x1, Pallas kernels, per_device(): pl.pallas_call(lambda *refs: transform_kernel(info, targets, tiles, *refs...  5.07 us
    pallas_call x1, Pallas kernels, per_device(): pl.pallas_call(lambda *refs: place_kernel(place_info, sources, tiles, *re...  2.86 us
  transfers between devices with their start and end apart: 18, of which 7 were waited for; matrix products, arithmetic and copies ran while one was open for 0% of the time, Pallas kernels for 0%

profile of v1, /device:TPU:0, one launch (start us, length us, event | category | flops | bytes accessed | tf_op | source)
XLA Modules:
  0.0 77.7 jit_solution(10889097274961227142)
XLA Ops:
  0.6 5.1 %transform.1 = (f32[264,128]{1,0:T(8,128)S(1)}, f32[264,128]{1,0:T(8,128)S(1)}, f32[264,128]{1,0:T(8,128)S(1)}, f32[264,128]{1,0:T(8,128)S(1)}, f32[264,128]{1,0...) custom-call(f32[4096,128]{1,0:T(8,128)} %bitcast.10, ...), custom_call_target="tpu_custom_call" | custom-call | tf_op jit(solution)/shard_map/transform/pallas_call | solution.py:330
  5.7 0.6 collective-permute-start
  6.3 3.6 %collective-permute-start.14 = (f32[136,128]{1,0:T(8,128)S(1)}, f32[136,128]{1,0:T(8,128)S(1)}, u32[]{:S(2)}, u32[]{:S(2)}) collective-permute-start(f32[136,128]{1,0:T(8,128)S(1)} %get-tuple-element.64), channel_id=1, source_target_pairs={{0,4},{1,5},{2,6},{3,7},{4,0},{5,1},{6,2},{7,3},{8,12},{9,13},{10,... | collective-permute-start | bytes 208904 | tf_op jit(solution)/shard_map/ppermute | solution.py:315
  10.0 0.1 join.1
  10.0 3.7 %collective-permute-start.1 = (f32[264,128]{1,0:T(8,128)S(1)}, f32[264,128]{1,0:T(8,128)S(1)}, u32[]{:S(2)}, u32[]{:S(2)}) collective-permute-start(f32[264,128]{1,0:T(8,128)S(1)} %get-tuple-element.51), channel_id=1, source_target_pairs={{0,6},{1,7},{2,4},{3,5},{4,2},{5,3},{6,0},{7,1},{8,14},{9,15},{10,... | collective-permute-start | bytes 405512 | tf_op jit(solution)/shard_map/ppermute | solution.py:315
  13.8 0.4 collective-permute-start.2
  14.1 3.4 %collective-permute-start.3 = (f32[264,128]{1,0:T(8,128)S(1)}, f32[264,128]{1,0:T(8,128)S(1)}, u32[]{:S(2)}, u32[]{:S(2)}) collective-permute-start(f32[264,128]{1,0:T(8,128)S(1)} %get-tuple-element.53), channel_id=1, source_target_pairs={{0,7},{1,6},{2,5},{3,4},{4,3},{5,2},{6,1},{7,0},{8,15},{9,14},{10,... | collective-permute-start | bytes 405512 | tf_op jit(solution)/shard_map/ppermute | solution.py:315
  17.6 1.0 %collective-permute-start.16 = (f32[136,128]{1,0:T(8,128)S(1)}, f32[136,128]{1,0:T(8,128)S(1)}, u32[]{:S(2)}, u32[]{:S(2)}) collective-permute-start(f32[136,128]{1,0:T(8,128)S(1)} %get-tuple-element.66), channel_id=1, source_target_pairs={{0,5},{1,4},{2,7},{3,6},{4,1},{5,0},{6,3},{7,2},{8,13},{9,12},{10,... | collective-permute-start | bytes 208904 | tf_op jit(solution)/shard_map/ppermute | solution.py:315
  18.6 7.0 %collective-permute-done.15.refs_17_ = f32[136,128]{1,0:T(8,128)S(1)} collective-permute-done((f32[136,128]{1,0:T(8,128)S(1)}, f32[136,128]{1,0:T(8,128)S(1)}, u32[]{:S(2)}, u32[]{:S(2)}) %collective-permute-start.15) | collective-permute-done | bytes 69664 | tf_op jit(solution)/shard_map/ppermute | solution.py:315
  25.6 14.8 %collective-permute-done.16.refs_18_ = f32[136,128]{1,0:T(8,128)S(1)} collective-permute-done((f32[136,128]{1,0:T(8,128)S(1)}, f32[136,128]{1,0:T(8,128)S(1)}, u32[]{:S(2)}, u32[]{:S(2)}) %collective-permute-start.16) | collective-permute-done | bytes 69664 | tf_op jit(solution)/shard_map/ppermute | solution.py:315
  40.4 0.5 collective-permute-start.4
  40.9 0.2 collective-permute-done.17.refs_19_
  41.1 7.7 %collective-permute-start.5 = (f32[264,128]{1,0:T(8,128)S(1)}, f32[264,128]{1,0:T(8,128)S(1)}, u32[]{:S(2)}, u32[]{:S(2)}) collective-permute-start(f32[264,128]{1,0:T(8,128)S(1)} %get-tuple-element.55), channel_id=1, source_target_pairs={{0,22},{1,23},{2,20},{3,21},{4,18},{5,19},{6,16},{7,17},{8,30},{9,... | collective-permute-start | bytes 405512 | tf_op jit(solution)/shard_map/ppermute | solution.py:315
  48.8 1.5 %collective-permute-start.7 = (f32[264,128]{1,0:T(8,128)S(1)}, f32[264,128]{1,0:T(8,128)S(1)}, u32[]{:S(2)}, u32[]{:S(2)}) collective-permute-start(f32[264,128]{1,0:T(8,128)S(1)} %get-tuple-element.57), channel_id=1, source_target_pairs={{0,1},{1,0},{2,3},{3,2},{4,5},{5,4},{6,7},{7,6},{8,9},{9,8},{10,11... | collective-permute-start | bytes 405512 | tf_op jit(solution)/shard_map/ppermute | solution.py:315
  50.3 5.0 %collective-permute-done.4.refs_4_ = f32[264,128]{1,0:T(8,128)S(1)} collective-permute-done((f32[264,128]{1,0:T(8,128)S(1)}, f32[264,128]{1,0:T(8,128)S(1)}, u32[]{:S(2)}, u32[]{:S(2)}) %collective-permute-start.4) | collective-permute-done | bytes 135200 | tf_op jit(solution)/shard_map/ppermute | solution.py:315
  55.2 3.5 %collective-permute-start.9 = (f32[264,128]{1,0:T(8,128)S(1)}, f32[264,128]{1,0:T(8,128)S(1)}, u32[]{:S(2)}, u32[]{:S(2)}) collective-permute-start(f32[264,128]{1,0:T(8,128)S(1)} %get-tuple-element.59), channel_id=1, source_target_pairs={{0,16},{1,17},{2,18},{3,19},{4,20},{5,21},{6,22},{7,23},{8,24},{9,... | collective-permute-start | bytes 405512 | tf_op jit(solution)/shard_map/ppermute | solution.py:315
  58.7 2.9 %collective-permute-start.10 = (f32[264,128]{1,0:T(8,128)S(1)}, f32[264,128]{1,0:T(8,128)S(1)}, u32[]{:S(2)}, u32[]{:S(2)}) collective-permute-start(f32[264,128]{1,0:T(8,128)S(1)} %get-tuple-element.60), channel_id=1, source_target_pairs={{0,3},{1,2},{2,1},{3,0},{4,7},{5,6},{6,5},{7,4},{8,11},{9,10},{10,... | collective-permute-start | bytes 405512 | tf_op jit(solution)/shard_map/ppermute | solution.py:315
  61.6 0.6 collective-permute-start.11
  62.2 4.3 %collective-permute-start.12 = (f32[264,128]{1,0:T(8,128)S(1)}, f32[264,128]{1,0:T(8,128)S(1)}, u32[]{:S(2)}, u32[]{:S(2)}) collective-permute-start(f32[264,128]{1,0:T(8,128)S(1)} %get-tuple-element.62), channel_id=1, source_target_pairs={{0,18},{1,19},{2,16},{3,17},{4,22},{5,23},{6,20},{7,21},{8,26},{9,... | collective-permute-start | bytes 405512 | tf_op jit(solution)/shard_map/ppermute | solution.py:315
  66.5 0.8 %collective-permute-start.13 = (f32[264,128]{1,0:T(8,128)S(1)}, f32[264,128]{1,0:T(8,128)S(1)}, u32[]{:S(2)}, u32[]{:S(2)}) collective-permute-start(f32[264,128]{1,0:T(8,128)S(1)} %get-tuple-element.63), channel_id=1, source_target_pairs={{0,19},{1,18},{2,17},{3,16},{4,23},{5,22},{6,21},{7,20},{8,27},{9,... | collective-permute-start | bytes 405512 | tf_op jit(solution)/shard_map/ppermute | solution.py:315
  67.3 3.9 %collective-permute-done.11.refs_11_ = f32[264,128]{1,0:T(8,128)S(1)} collective-permute-done((f32[264,128]{1,0:T(8,128)S(1)}, f32[264,128]{1,0:T(8,128)S(1)}, u32[]{:S(2)}, u32[]{:S(2)}) %collective-permute-start.11) | collective-permute-done | bytes 135200 | tf_op jit(solution)/shard_map/ppermute | solution.py:315
  71.3 1.5 %collective-permute-done.12.refs_12_ = f32[264,128]{1,0:T(8,128)S(1)} collective-permute-done((f32[264,128]{1,0:T(8,128)S(1)}, f32[264,128]{1,0:T(8,128)S(1)}, u32[]{:S(2)}, u32[]{:S(2)}) %collective-permute-start.12) | collective-permute-done | bytes 135200 | tf_op jit(solution)/shard_map/ppermute | solution.py:315
  72.7 2.1 %collective-permute-done.13.refs_13_ = f32[264,128]{1,0:T(8,128)S(1)} collective-permute-done((f32[264,128]{1,0:T(8,128)S(1)}, f32[264,128]{1,0:T(8,128)S(1)}, u32[]{:S(2)}, u32[]{:S(2)}) %collective-permute-start.13) | collective-permute-done | bytes 135200 | tf_op jit(solution)/shard_map/ppermute | solution.py:315
  74.9 2.9 %place.1 = (f32[4096,128]{1,0:T(8,128)}, f32[3]{0:T(128)}) custom-call(bf16[128,256]{1,0:T(8,128)(2,1)S(1)} %copy-done, f32[264,128]{1,0:T(8,128)S(1)} %collective-permute-done.1.refs_1_, f32[264,128]{1,0:T(8,128)S(1)} %collective-permute-done.2.refs_2_, f32[264,128]{1,0:T(8,128)S(1)} %collective-permute-done.3.refs_3_, ...), custom_call_target="tpu_custom_call" | custom-call | tf_op jit(solution)/shard_map/place/pallas_call | solution.py:369
  (17 shorter events, 0.1 us)
Async XLA Ops:
  5.7 69.2 %copy-start = (bf16[128,256]{1,0:T(8,128)(2,1)S(1)}, bf16[128,256]{1,0:T(8,128)(2,1)}, u32[]{:S(2)}) copy-start(bf16[128,256]{1,0:T(8,128)(2,1)} %constant.11.clone.refs_0_) | copy-start | bytes 196612
  5.7 4.3 %collective-permute-start = (f32[1800,128]{1,0:T(8,128)S(1)}, f32[1800,128]{1,0:T(8,128)S(1)}, u32[]{:S(2)}, u32[]{:S(2)}) collective-permute-start(f32[1800,128]{1,0:T(8,128)S(1)} %get-tuple-element.36), channel_id=1, source_target_pairs={{0,8},{1,9},{2,10},{3,11},{4,12},{5,13},{6,14},{7,15},{8,0},{9,1},... | collective-permute-start | bytes 2764808 | tf_op jit(solution)/shard_map/ppermute | solution.py:315
  6.3 11.3 %collective-permute-start.14 = (f32[136,128]{1,0:T(8,128)S(1)}, f32[136,128]{1,0:T(8,128)S(1)}, u32[]{:S(2)}, u32[]{:S(2)}) collective-permute-start(f32[136,128]{1,0:T(8,128)S(1)} %get-tuple-element.64), channel_id=1, source_target_pairs={{0,4},{1,5},{2,6},{3,7},{4,0},{5,1},{6,2},{7,3},{8,12},{9,13},{10,... | collective-permute-start | bytes 208904 | tf_op jit(solution)/shard_map/ppermute | solution.py:315
  9.9 15.7 %collective-permute-start.15 = (f32[136,128]{1,0:T(8,128)S(1)}, f32[136,128]{1,0:T(8,128)S(1)}, u32[]{:S(2)}, u32[]{:S(2)}) collective-permute-start(f32[136,128]{1,0:T(8,128)S(1)} %get-tuple-element.65), channel_id=1, source_target_pairs={{0,12},{1,13},{2,14},{3,15},{4,8},{5,9},{6,10},{7,11},{8,4},{9,5},... | collective-permute-start | bytes 208904 | tf_op jit(solution)/shard_map/ppermute | solution.py:315
  10.0 38.8 %collective-permute-start.1 = (f32[264,128]{1,0:T(8,128)S(1)}, f32[264,128]{1,0:T(8,128)S(1)}, u32[]{:S(2)}, u32[]{:S(2)}) collective-permute-start(f32[264,128]{1,0:T(8,128)S(1)} %get-tuple-element.51), channel_id=1, source_target_pairs={{0,6},{1,7},{2,4},{3,5},{4,2},{5,3},{6,0},{7,1},{8,14},{9,15},{10,... | collective-permute-start | bytes 405512 | tf_op jit(solution)/shard_map/ppermute | solution.py:315
  13.8 35.1 %collective-permute-start.2 = (f32[264,128]{1,0:T(8,128)S(1)}, f32[264,128]{1,0:T(8,128)S(1)}, u32[]{:S(2)}, u32[]{:S(2)}) collective-permute-start(f32[264,128]{1,0:T(8,128)S(1)} %get-tuple-element.52), channel_id=1, source_target_pairs={{0,20},{1,21},{2,22},{3,23},{4,16},{5,17},{6,18},{7,19},{8,28},{9,... | collective-permute-start | bytes 405512 | tf_op jit(solution)/shard_map/ppermute | solution.py:315
  14.1 36.1 %collective-permute-start.3 = (f32[264,128]{1,0:T(8,128)S(1)}, f32[264,128]{1,0:T(8,128)S(1)}, u32[]{:S(2)}, u32[]{:S(2)}) collective-permute-start(f32[264,128]{1,0:T(8,128)S(1)} %get-tuple-element.53), channel_id=1, source_target_pairs={{0,7},{1,6},{2,5},{3,4},{4,3},{5,2},{6,1},{7,0},{8,15},{9,14},{10,... | collective-permute-start | bytes 405512 | tf_op jit(solution)/shard_map/ppermute | solution.py:315
  17.6 22.8 %collective-permute-start.16 = (f32[136,128]{1,0:T(8,128)S(1)}, f32[136,128]{1,0:T(8,128)S(1)}, u32[]{:S(2)}, u32[]{:S(2)}) collective-permute-start(f32[136,128]{1,0:T(8,128)S(1)} %get-tuple-element.66), channel_id=1, source_target_pairs={{0,5},{1,4},{2,7},{3,6},{4,1},{5,0},{6,3},{7,2},{8,13},{9,12},{10,... | collective-permute-start | bytes 208904 | tf_op jit(solution)/shard_map/ppermute | solution.py:315
  25.6 15.5 %collective-permute-start.17 = (f32[136,128]{1,0:T(8,128)S(1)}, f32[136,128]{1,0:T(8,128)S(1)}, u32[]{:S(2)}, u32[]{:S(2)}) collective-permute-start(f32[136,128]{1,0:T(8,128)S(1)} %get-tuple-element.67), channel_id=1, source_target_pairs={{0,13},{1,12},{2,15},{3,14},{4,9},{5,8},{6,11},{7,10},{8,5},{9,4},... | collective-permute-start | bytes 208904 | tf_op jit(solution)/shard_map/ppermute | solution.py:315
  40.4 14.9 %collective-permute-start.4 = (f32[264,128]{1,0:T(8,128)S(1)}, f32[264,128]{1,0:T(8,128)S(1)}, u32[]{:S(2)}, u32[]{:S(2)}) collective-permute-start(f32[264,128]{1,0:T(8,128)S(1)} %get-tuple-element.54), channel_id=1, source_target_pairs={{0,21},{1,20},{2,23},{3,22},{4,17},{5,16},{6,19},{7,18},{8,29},{9,... | collective-permute-start | bytes 405512 | tf_op jit(solution)/shard_map/ppermute | solution.py:315
  41.1 17.6 %collective-permute-start.5 = (f32[264,128]{1,0:T(8,128)S(1)}, f32[264,128]{1,0:T(8,128)S(1)}, u32[]{:S(2)}, u32[]{:S(2)}) collective-permute-start(f32[264,128]{1,0:T(8,128)S(1)} %get-tuple-element.55), channel_id=1, source_target_pairs={{0,22},{1,23},{2,20},{3,21},{4,18},{5,19},{6,16},{7,17},{8,30},{9,... | collective-permute-start | bytes 405512 | tf_op jit(solution)/shard_map/ppermute | solution.py:315
  48.8 12.8 %collective-permute-start.6 = (f32[264,128]{1,0:T(8,128)S(1)}, f32[264,128]{1,0:T(8,128)S(1)}, u32[]{:S(2)}, u32[]{:S(2)}) collective-permute-start(f32[264,128]{1,0:T(8,128)S(1)} %get-tuple-element.56), channel_id=1, source_target_pairs={{0,23},{1,22},{2,21},{3,20},{4,19},{5,18},{6,17},{7,16},{8,31},{9,... | collective-permute-start | bytes 405512 | tf_op jit(solution)/shard_map/ppermute | solution.py:315
  48.8 13.4 %collective-permute-start.7 = (f32[264,128]{1,0:T(8,128)S(1)}, f32[264,128]{1,0:T(8,128)S(1)}, u32[]{:S(2)}, u32[]{:S(2)}) collective-permute-start(f32[264,128]{1,0:T(8,128)S(1)} %get-tuple-element.57), channel_id=1, source_target_pairs={{0,1},{1,0},{2,3},{3,2},{4,5},{5,4},{6,7},{7,6},{8,9},{9,8},{10,11... | collective-permute-start | bytes 405512 | tf_op jit(solution)/shard_map/ppermute | solution.py:315
  50.3 16.2 %collective-permute-start.8 = (f32[264,128]{1,0:T(8,128)S(1)}, f32[264,128]{1,0:T(8,128)S(1)}, u32[]{:S(2)}, u32[]{:S(2)}) collective-permute-start(f32[264,128]{1,0:T(8,128)S(1)} %get-tuple-element.58), channel_id=1, source_target_pairs={{0,2},{1,3},{2,0},{3,1},{4,6},{5,7},{6,4},{7,5},{8,10},{9,11},{10,... | collective-permute-start | bytes 405512 | tf_op jit(solution)/shard_map/ppermute | solution.py:315
  55.2 12.1 %collective-permute-start.9 = (f32[264,128]{1,0:T(8,128)S(1)}, f32[264,128]{1,0:T(8,128)S(1)}, u32[]{:S(2)}, u32[]{:S(2)}) collective-permute-start(f32[264,128]{1,0:T(8,128)S(1)} %get-tuple-element.59), channel_id=1, source_target_pairs={{0,16},{1,17},{2,18},{3,19},{4,20},{5,21},{6,22},{7,23},{8,24},{9,... | collective-permute-start | bytes 405512 | tf_op jit(solution)/shard_map/ppermute | solution.py:315
  58.7 8.6 %collective-permute-start.10 = (f32[264,128]{1,0:T(8,128)S(1)}, f32[264,128]{1,0:T(8,128)S(1)}, u32[]{:S(2)}, u32[]{:S(2)}) collective-permute-start(f32[264,128]{1,0:T(8,128)S(1)} %get-tuple-element.60), channel_id=1, source_target_pairs={{0,3},{1,2},{2,1},{3,0},{4,7},{5,6},{6,5},{7,4},{8,11},{9,10},{10,... | collective-permute-start | bytes 405512 | tf_op jit(solution)/shard_map/ppermute | solution.py:315
  61.6 9.6 %collective-permute-start.11 = (f32[264,128]{1,0:T(8,128)S(1)}, f32[264,128]{1,0:T(8,128)S(1)}, u32[]{:S(2)}, u32[]{:S(2)}) collective-permute-start(f32[264,128]{1,0:T(8,128)S(1)} %get-tuple-element.61), channel_id=1, source_target_pairs={{0,17},{1,16},{2,19},{3,18},{4,21},{5,20},{6,23},{7,22},{8,25},{9,... | collective-permute-start | bytes 405512 | tf_op jit(solution)/shard_map/ppermute | solution.py:315
  62.2 10.6 %collective-permute-start.12 = (f32[264,128]{1,0:T(8,128)S(1)}, f32[264,128]{1,0:T(8,128)S(1)}, u32[]{:S(2)}, u32[]{:S(2)}) collective-permute-start(f32[264,128]{1,0:T(8,128)S(1)} %get-tuple-element.62), channel_id=1, source_target_pairs={{0,18},{1,19},{2,16},{3,17},{4,22},{5,23},{6,20},{7,21},{8,26},{9,... | collective-permute-start | bytes 405512 | tf_op jit(solution)/shard_map/ppermute | solution.py:315
  66.5 8.4 %collective-permute-start.13 = (f32[264,128]{1,0:T(8,128)S(1)}, f32[264,128]{1,0:T(8,128)S(1)}, u32[]{:S(2)}, u32[]{:S(2)}) collective-permute-start(f32[264,128]{1,0:T(8,128)S(1)} %get-tuple-element.63), channel_id=1, source_target_pairs={{0,19},{1,18},{2,17},{3,16},{4,23},{5,22},{6,21},{7,20},{8,27},{9,... | collective-permute-start | bytes 405512 | tf_op jit(solution)/shard_map/ppermute | solution.py:315

commit v2 on v1

--- a/solution.py
+++ b/solution.py
@@ -15,6 +15,7 @@
 RADIX = 2**WINDOW // LANES
 AXES = ("outer", "inner")
 VMEM_LIMIT = 16 * 2**20
+SUB = 32
 
 
 def flip(value, count):
@@ -30,7 +31,7 @@
     return high, low
 
 
-def transform_tables():
+def transform_tables(n_devices):
     columns = 2**WINDOW
     freq = np.arange(LANES) * RADIX
     sample = np.arange(LANES)
@@ -40,8 +41,20 @@
         cosine = np.cos(angles) / math.sqrt(columns)
         sine = np.sin(angles) / math.sqrt(columns)
         rows = np.stack([np.concatenate([cosine, -sine], 1), np.concatenate([sine, cosine], 1)], 1)
-        tables.append(rows.reshape(2 * LANES, 2 * LANES))
-    return split_halves(np.stack(tables))
+        tables.append(rows.reshape(n_devices // 2, 2, 8, 2 * LANES))
+    high, low = split_halves(np.stack(tables))
+    both = np.concatenate([high, low], 0).transpose(1, 0, 2, 3, 4)
+    both = np.stack([both, both[:, :, ::-1]])
+    return both.reshape(2, n_devices // 2, 2 * RADIX, 16, 2 * LANES)
+
+
+def phase_tables(chunks, n_devices, angle_scale):
+    turn = np.array([flip(row, LANES.bit_length() - 1) for row in range(LANES)])
+    angles = turn * float(chunks * n_devices) * angle_scale
+    table = np.zeros((2, LANES, LANES))
+    table[0, :, 1] = np.cos(angles)
+    table[1, :, 1] = np.sin(angles)
+    return table.astype(np.float32)
 
 
 def halves(values):
@@ -56,9 +69,9 @@
     )
 
 
-def transform_kernel(info, targets, tiles, x_hbm, high_hbm, low_hbm, order_hbm, *refs):
+def transform_kernel(info, targets, tiles, x_hbm, table_hbm, phase_hbm, *refs):
     n_devices, chunks, angle_scale, device_id = info()
-    outs, (x_ref, high_ref, low_ref, order_ref, stage, sems) = refs[:-6], refs[-6:]
+    outs, (x_ref, table_ref, phase_ref, high_ref, low_ref, sems) = refs[:-6], refs[-6:]
     chunk_rows = RADIX * 8
     x_rows = x_ref.shape[0] // chunks
     dev_bits = n_devices.bit_length() - 1
@@ -71,80 +84,99 @@
     for chunk in range(chunks):
         rows = pl.ds(chunk * x_rows, x_rows)
         loads.append(load(x_hbm.at[rows], x_ref.at[rows], chunk))
-    sides = [load(order_hbm, order_ref, chunks)]
-    tables = []
-    for residue in range(RADIX):
-        index = chunks + 1 + 2 * residue
-        tables.append(
-            [
-                load(high_hbm.at[residue], high_ref.at[residue], index),
-                load(low_hbm.at[residue], low_ref.at[residue], index + 1),
-            ]
+    phase_load = load(phase_hbm, phase_ref, chunks)
+    table_loads = [
+        load(
+            table_hbm.at[device_id & 1, (device_id >> 1) ^ block],
+            table_ref.at[block],
+            chunks + 1 + block,
         )
-    for copy in loads[:1] + sides + sum(tables, []) + loads[1:]:
+        for block in range(n_devices // 2)
+    ]
+    for copy in loads[:1] + [phase_load] + loads[1:2] + table_loads + loads[2:]:
         copy.start()
 
     base = jnp.int32(0)
     for bit in range(dev_bits):
         base += (device_id >> bit & 1) << (dev_bits - 1 - bit)
-    lane = lax.broadcasted_iota(jnp.int32, (LANES, LANES), 1)
     square_sum = real_sum = imag_sum = jnp.zeros((8, LANES), jnp.float32)
-    for chunk in range(chunks):
-        loads[chunk].wait()
-        parts = [
-            [
-                x_ref[pl.ds(chunk * x_rows + 2 * j + s, LANES, stride=2 * RADIX), :]
-                for s in range(2)
-            ]
-            for j in range(RADIX)
-        ]
-        squares = sum(p * p for pair in parts for p in pair)
-        square_sum += squares.reshape(LANES // 8, 8, LANES).sum(0)
-
-        if chunk == 0:
-            sides[0].wait()
-        offset = (base + n_devices * flip(chunk, chunk_bits)).astype(jnp.float32)
-        theta = (order_ref[...] * float(n_devices * chunks) + offset) * angle_scale
-        theta_sq = theta * theta
-        cosine = 1.0 - theta_sq * (0.5 - theta_sq * (1.0 / 24.0))
-        sine = theta * (1.0 - theta_sq * (1.0 / 6.0 - theta_sq * (1.0 / 120.0)))
-        cosine = jnp.where(lane == 1, cosine, 0.0)
-        sine = jnp.where(lane == 1, sine, 0.0)
-        first_re, first_im = parts[0]
-        real_terms = first_re * cosine + first_im * sine
-        imag_terms = first_im * cosine - first_re * sine
-        real_sum += real_terms.reshape(LANES // 8, 8, LANES).sum(0)
-        imag_sum += imag_terms.reshape(LANES // 8, 8, LANES).sum(0)
-
-        (r0, i0), (r1, i1), (r2, i2), (r3, i3) = parts
-        ar, ai, br, bi = r0 + r2, i0 + i2, r0 - r2, i0 - i2
-        cr, ci, dr, di = r1 + r3, i1 + i3, r1 - r3, i1 - i3
-        folded = [(ar + cr, ai + ci), (br - di, bi + dr), (ar - cr, ai - ci), (br + di, bi - dr)]
+    fold = lambda value: value.reshape(SUB // 8, 8, LANES).sum(0)
+    for half in range(chunks // 2):
+        for chunk in (2 * half, 2 * half + 1):
+            loads[chunk].wait()
+            if chunk == 0:
+                phase_load.wait()
+            turn_re = turn_im = jnp.zeros((8, LANES), jnp.float32)
+            for sub in range(LANES // SUB):
+                start = chunk * x_rows + sub * SUB * 2 * RADIX
+                parts = [
+                    [x_ref[pl.ds(start + 2 * j + s, SUB, stride=2 * RADIX), :] for s in range(2)]
+                    for j in range(RADIX)
+                ]
+                square_sum += fold(sum(p * p for pair in parts for p in pair))
+                cosine = phase_ref[0, sub * SUB : (sub + 1) * SUB]
+                sine = phase_ref[1, sub * SUB : (sub + 1) * SUB]
+                first_re, first_im = parts[0]
+                turn_re += fold(first_re * cosine + first_im * sine)
+                turn_im += fold(first_im * cosine - first_re * sine)
+                (r0, i0), (r1, i1), (r2, i2), (r3, i3) = parts
+                ar, ai, br, bi = r0 + r2, i0 + i2, r0 - r2, i0 - i2
+                cr, ci, dr, di = r1 + r3, i1 + i3, r1 - r3, i1 - i3
+                folded = [
+                    (ar + cr, ai + ci),
+                    (br - di, bi + dr),
+                    (ar - cr, ai - ci),
+                    (br + di, bi - dr),
+                ]
+                row = (chunk % 2) * LANES + sub * SUB
+                for residue in range(RADIX):
+                    for part in range(2):
+                        high, low = halves(folded[residue][part])
+                        where = (residue, pl.ds(row, SUB), pl.ds(part * LANES, LANES))
+                        high_ref[where] = high
+                        low_ref[where] = low
+            angle = flip(chunk, chunk_bits) * n_devices * angle_scale
+            cosine, sine = math.cos(angle), math.sin(angle)
+            real_sum += turn_re * cosine + turn_im * sine
+            imag_sum += turn_im * cosine - turn_re * sine
+        if half == 0:
+            for copy in table_loads:
+                copy.wait()
         for residue in range(RADIX):
-            high, low = halves(jnp.concatenate(folded[residue], 1))
-            if chunk == 0:
-                for copy in tables[residue]:
-                    copy.wait()
-            table = high_ref[residue]
-            values = dot_rows(table, high) + dot_rows(table, low) + dot_rows(low_ref[residue], high)
-            stage[:, residue * 8 : residue * 8 + 8, :] = values.reshape(n_devices, 8, LANES)
-        for mask, out, row in targets:
-            rows = pl.ds(row + chunk * chunk_rows, chunk_rows)
-            outs[out][rows, :] = stage[device_id ^ mask]
-
-    sums = [value.sum(0, keepdims=True) for value in (square_sum, real_sum, imag_sum)]
+            table_high = table_ref[:, residue].reshape(2 * LANES, 2 * LANES)
+            table_low = table_ref[:, RADIX + residue].reshape(2 * LANES, 2 * LANES)
+            high, low = high_ref[residue], low_ref[residue]
+            values = dot_rows(table_high, high) + dot_rows(table_high, low)
+            values += dot_rows(table_low, high)
+            for mask, out, row in targets:
+                for part in range(2):
+                    rows = pl.ds(row + (2 * half + part) * chunk_rows + residue * 8, 8)
+                    outs[out][rows, :] = values[
+                        8 * mask : 8 * mask + 8, part * LANES : (part + 1) * LANES
+                    ]
+
+    theta = jnp.full((8, LANES), base, jnp.int32).astype(jnp.float32) * angle_scale
+    theta_sq = theta * theta
+    cosine = 1.0 - theta_sq * (0.5 - theta_sq * (1.0 / 24.0))
+    sine = theta * (1.0 - theta_sq * (1.0 / 6.0 - theta_sq * (1.0 / 120.0)))
+    turned = (square_sum, real_sum * cosine + imag_sum * sine, imag_sum * cosine - real_sum * sine)
+    sums = [value.sum(0, keepdims=True) for value in turned]
     tile = jnp.concatenate(sums + [jnp.zeros((5, LANES), jnp.float32)], 0)
     for out, row in tiles:
         outs[out][pl.ds(row, 8), :] = tile
 
 
-def join_kernel(plan, n_join, swapped_ref, own_ref, *refs):
-    outs = refs[n_join:]
-    rows, tile_row = plan
-    tile = swapped_ref[pl.ds(tile_row, 8), :] + own_ref[pl.ds(rows, 8), :]
-    for index in range(n_join):
-        outs[index][pl.ds(rows, rows), :] = swapped_ref[pl.ds(index * rows, rows), :]
-        outs[index][pl.ds(2 * rows, 8), :] = tile
+def join_kernel(rows, first, stamps, n_join, swapped_ref, *refs):
+    refs = (swapped_ref,) + refs
+    outs = refs[len(refs) - n_join :]
+    tile = None
+    for operand, row in stamps:
+        value = refs[operand][pl.ds(row, 8), :]
+        tile = value if tile is None else tile + value
+    for index, out in enumerate(outs):
+        out[pl.ds(rows, rows), :] = swapped_ref[pl.ds((first + index) * rows, rows), :]
+        if tile is not None:
+            out[pl.ds(2 * rows, 8), :] = tile
 
 
 def place_kernel(info, sources, tiles, order_ref, *refs):
@@ -287,11 +319,12 @@
     vectors = 2 * amp_dev // LANES
     slot_rows = chunks * RADIX * 8 + 8
     x = amplitudes.reshape(2, vectors // 2, LANES).transpose(1, 0, 2).reshape(vectors, LANES)
-    high, low = transform_tables()
+    angle_scale = 2.0 * math.pi / total_len
+    table = transform_tables(n_devices)
+    phase = phase_tables(chunks, n_devices, angle_scale)
     turn = np.array([flip(lane, LANES.bit_length() - 1) for lane in range(LANES)])
     order = (turn[:, None] == np.arange(LANES)[None, :]).astype(np.float32)
     order = np.concatenate([order, order], 1).astype(ml_dtypes.bfloat16)
-    turn_table = np.broadcast_to(turn[:, None], (LANES, LANES)).astype(np.float32)
 
     rows = chunks * RADIX * 8
     core_bit = n_inner
@@ -300,12 +333,13 @@
     chip_masks = [mask for mask in range(n_devices) if not mask & core_bit]
     far = sorted([mask for mask in chip_masks if mask & far_bit], key=weight)
     near = sorted([mask for mask in chip_masks if mask and not mask & far_bit], key=weight)
-    direct, pairs = far[:2], far[2:] + near
+    direct, far = far[:2], far[2:]
+    pairs = far + near
     n_pairs = len(pairs)
 
     def info():
         device_id = lax.axis_index("outer") * n_inner + lax.axis_index("inner")
-        return n_devices, chunks, 2.0 * math.pi / total_len, device_id
+        return n_devices, chunks, angle_scale, device_id
 
     def place_info():
         return n_devices, chunks, total_len, info()[3]
@@ -316,46 +350,55 @@
 
     singles = [mask ^ core for mask in direct for core in (0, core_bit)]
     swap_rows = (n_pairs + 1) * rows
-    shapes = [(2 * rows + 8, LANES)] * n_pairs + [(rows + 8, LANES), (swap_rows + 8, LANES)]
-    shapes += [(rows + 8, LANES)] * len(singles)
+    pair_rows = [2 * rows] * len(far) + [2 * rows + 8] * len(near)
+    single_rows = [rows + 8] * 2 + [rows] * (len(singles) - 2)
+    all_rows = pair_rows + [rows + 8, swap_rows + 8] + single_rows
     stay, swap = n_pairs, n_pairs + 1
     targets = [(mask, index, 0) for index, mask in enumerate(pairs)] + [(0, stay, 0)]
     targets += [(mask ^ core_bit, swap, index * rows) for index, mask in enumerate(pairs + [0])]
     targets += [(mask, swap + 1 + index, 0) for index, mask in enumerate(singles)]
-    tiles = [(stay, rows), (swap, swap_rows)]
-    tiles += [(swap + 1 + index, rows) for index in range(len(singles))]
+    tiles = [(stay, rows), (swap, swap_rows), (swap + 1, rows), (swap + 2, rows)]
+    constrain = lambda value: pltpu.with_memory_space_constraint(value, pltpu.HBM)
+    shaped = lambda count: jax.ShapeDtypeStruct((count, LANES), jnp.float32)
     whole = lambda shape: pl.BlockSpec(shape, lambda i: (0,) * len(shape))
     hbm = pl.BlockSpec(memory_space=pltpu.HBM)
     vmem = pl.BlockSpec(memory_space=pltpu.VMEM)
     sent = pl.pallas_call(
         lambda *refs: transform_kernel(info, targets, tiles, *refs),
-        in_specs=[hbm] * 4,
-        out_specs=[vmem] * len(shapes),
-        out_shape=[jax.ShapeDtypeStruct(shape, jnp.float32) for shape in shapes],
+        in_specs=[hbm] * 3,
+        out_specs=[vmem] * len(all_rows),
+        out_shape=[shaped(count) for count in all_rows],
         scratch_shapes=[
             pltpu.VMEM((vectors, LANES), jnp.float32),
-            pltpu.VMEM(high.shape, jnp.bfloat16),
-            pltpu.VMEM(low.shape, jnp.bfloat16),
-            pltpu.VMEM(turn_table.shape, jnp.float32),
-            pltpu.VMEM((n_devices, RADIX * 8, LANES), jnp.float32),
-            pltpu.SemaphoreType.DMA((chunks + 1 + 2 * RADIX,)),
+            pltpu.VMEM(table.shape[1:], jnp.bfloat16),
+            pltpu.VMEM(phase.shape, jnp.float32),
+            pltpu.VMEM((RADIX, 2 * LANES, 2 * LANES), jnp.bfloat16),
+            pltpu.VMEM((RADIX, 2 * LANES, 2 * LANES), jnp.bfloat16),
+            pltpu.SemaphoreType.DMA((chunks + 1 + n_devices // 2,)),
         ],
         compiler_params=pltpu.CompilerParams(vmem_limit_bytes=VMEM_LIMIT),
         name="transform",
-    )(*[pltpu.with_memory_space_constraint(a, pltpu.HBM) for a in (x, jnp.asarray(high), jnp.asarray(low), jnp.asarray(turn_table))])
+    )(constrain(x), constrain(jnp.asarray(table)), constrain(jnp.asarray(phase)))
     swapped = exchange(sent[swap], core_bit)
     arrived_singles = []
     for index, mask in enumerate(singles):
         arrived_singles.append(exchange(sent[swap + 1 + index], mask))
-    joined = pl.pallas_call(
-        lambda *refs: join_kernel((rows, swap_rows), n_pairs, *refs),
-        in_specs=[vmem] * (2 + n_pairs),
-        out_specs=[vmem] * n_pairs,
-        out_shape=[jax.ShapeDtypeStruct(shapes[0], jnp.float32)] * n_pairs,
-        input_output_aliases={2 + i: i for i in range(n_pairs)},
-        compiler_params=pltpu.CompilerParams(vmem_limit_bytes=VMEM_LIMIT),
-        name="join",
-    )(swapped, sent[stay], *sent[:n_pairs])
+
+    def join(first, count, extra, stamps):
+        n_extra = len(extra)
+        return pl.pallas_call(
+            lambda *refs: join_kernel(rows, first, stamps, count, *refs),
+            in_specs=[vmem] * (1 + n_extra + count),
+            out_specs=[vmem] * count,
+            out_shape=[shaped(size) for size in pair_rows[first : first + count]],
+            input_output_aliases={1 + n_extra + i: i for i in range(count)},
+            compiler_params=pltpu.CompilerParams(vmem_limit_bytes=VMEM_LIMIT),
+            name="join",
+        )(swapped, *extra, *sent[first : first + count])
+
+    joined = join(0, len(far), [], [])
+    stamps = [(0, swap_rows), (1, rows), (2, rows), (3, rows)]
+    joined += join(len(far), len(near), [sent[stay]] + arrived_singles[:2], stamps)
     arrived_pairs = []
     for index, mask in enumerate(pairs):
         arrived_pairs.append(exchange(joined[index], mask))
@@ -365,9 +408,9 @@
         sources += [(mask, index, 0), (mask ^ core_bit, index, rows)]
     sources += [(0, stay, 0), (core_bit, swap, n_pairs * rows)]
     sources += [(mask, swap + 1 + index, 0) for index, mask in enumerate(singles)]
-    tiles = [(index, 2 * rows) for index in range(n_pairs)] + tiles
+    sums = tiles + [(len(far) + index, 2 * rows) for index in range(len(near))]
     placed, checks = pl.pallas_call(
-        lambda *refs: place_kernel(place_info, sources, tiles, *refs),
+        lambda *refs: place_kernel(place_info, sources, sums, *refs),
         grid=(groups,),
         in_specs=[whole(order.shape)] + [vmem] * len(arrivals),
         out_specs=[

time: 77.9 us -> 75.3 us (0.967)
  Pallas kernels: 7.99 us -> 6.12 us
  starting transfers between devices: 34.5 us -> 32.9 us
    pallas_call x1, Pallas kernels: 5.07 us -> 3.2 us  [per_device(): pl.pallas_call(lambda *refs: transform_kernel(info, targets, tiles, *refs...]
    ppermute x18, starting transfers between devices: 34.5 us -> 32.9 us  [exchange(): return lax.ppermute(values, AXES, pairs_of)]
    pallas_call x2 -> x3, Pallas kernels: 2.92 us -> 2.91 us  [the longest x1 2.85 us: per_device(): pl.pallas_call(lambda *refs: place_kernel(place_info, sources, sums, *ref...]
where the time goes in v2:
time: 75.3 us; the launch traced here: 74.9 us
  waiting for transfers between devices  35.2 us (47%)
  starting transfers between devices  32.9 us (44%)
  Pallas kernels  6.12 us (8%)
    ppermute x18, waiting for transfers between devices, exchange(): return lax.ppermute(values, AXES, pairs_of)  35.2 us
    ppermute x18, starting transfers between devices, exchange(): return lax.ppermute(values, AXES, pairs_of)  32.9 us
    pallas_call x1, Pallas kernels, per_device(): pl.pallas_call(lambda *refs: transform_kernel(info, targets, tiles, *refs...  3.2 us
    pallas_call x1, Pallas kernels, per_device(): pl.pallas_call(lambda *refs: place_kernel(place_info, sources, sums, *ref...  2.85 us
  transfers between devices with their start and end apart: 18, of which 7 were waited for; matrix products, arithmetic and copies ran while one was open for 0% of the time, Pallas kernels for 0%

profile of v2, /device:TPU:0, one launch (start us, length us, event | category | flops | bytes accessed | tf_op | source)
XLA Modules:
  0.0 74.9 jit_solution(4726550853383605427)
XLA Ops:
  0.6 3.2 %transform.1 = (f32[256,128]{1,0:T(8,128)S(1)}, f32[256,128]{1,0:T(8,128)S(1)}, f32[256,128]{1,0:T(8,128)S(1)}, f32[256,128]{1,0:T(8,128)S(1)}, f32[256,128]{1,0...) custom-call(f32[4096,128]{1,0:T(8,128)} %bitcast.10, ...), custom_call_target="tpu_custom_call" | custom-call | tf_op jit(solution)/shard_map/transform/pallas_call | solution.py:366
  3.9 0.6 collective-permute-start
  4.4 3.7 %collective-permute-start.7 = (f32[136,128]{1,0:T(8,128)S(1)}, f32[136,128]{1,0:T(8,128)S(1)}, u32[]{:S(2)}, u32[]{:S(2)}) collective-permute-start(f32[136,128]{1,0:T(8,128)S(1)} %get-tuple-element.50), channel_id=1, source_target_pairs={{0,4},{1,5},{2,6},{3,7},{4,0},{5,1},{6,2},{7,3},{8,12},{9,13},{10,... | collective-permute-start | bytes 208904 | tf_op jit(solution)/shard_map/ppermute | solution.py:349
  8.1 3.7 %collective-permute-start.1 = (f32[256,128]{1,0:T(8,128)S(1)}, f32[256,128]{1,0:T(8,128)S(1)}, u32[]{:S(2)}, u32[]{:S(2)}) collective-permute-start(f32[256,128]{1,0:T(8,128)S(1)} %get-tuple-element.43), channel_id=1, source_target_pairs={{0,6},{1,7},{2,4},{3,5},{4,2},{5,3},{6,0},{7,1},{8,14},{9,15},{10,... | collective-permute-start | bytes 393224 | tf_op jit(solution)/shard_map/ppermute | solution.py:349
  11.9 0.4 collective-permute-start.2
  12.2 3.4 %collective-permute-start.3 = (f32[256,128]{1,0:T(8,128)S(1)}, f32[256,128]{1,0:T(8,128)S(1)}, u32[]{:S(2)}, u32[]{:S(2)}) collective-permute-start(f32[256,128]{1,0:T(8,128)S(1)} %get-tuple-element.45), channel_id=1, source_target_pairs={{0,7},{1,6},{2,5},{3,4},{4,3},{5,2},{6,1},{7,0},{8,15},{9,14},{10,... | collective-permute-start | bytes 393224 | tf_op jit(solution)/shard_map/ppermute | solution.py:349
  15.7 1.0 %collective-permute-start.16 = (f32[128,128]{1,0:T(8,128)S(1)}, f32[128,128]{1,0:T(8,128)S(1)}, u32[]{:S(2)}, u32[]{:S(2)}) collective-permute-start(f32[128,128]{1,0:T(8,128)S(1)} %get-tuple-element.66), channel_id=1, source_target_pairs={{0,5},{1,4},{2,7},{3,6},{4,1},{5,0},{6,3},{7,2},{8,13},{9,12},{10,... | collective-permute-start | bytes 196616 | tf_op jit(solution)/shard_map/ppermute | solution.py:349
  16.7 6.8 %collective-permute-done.8.refs_3_.refs_17_ = f32[136,128]{1,0:T(8,128)S(1)} collective-permute-done((f32[136,128]{1,0:T(8,128)S(1)}, f32[136,128]{1,0:T(8,128)S(1)}, u32[]{:S(2)}, u32[]{:S(2)}) %collective-permute-start.8) | collective-permute-done | bytes 69664 | tf_op jit(solution)/shard_map/ppermute | solution.py:349
  23.5 14.2 %collective-permute-done.16.refs_18_ = f32[128,128]{1,0:T(8,128)S(1)} collective-permute-done((f32[128,128]{1,0:T(8,128)S(1)}, f32[128,128]{1,0:T(8,128)S(1)}, u32[]{:S(2)}, u32[]{:S(2)}) %collective-permute-start.16) | collective-permute-done | bytes 65568 | tf_op jit(solution)/shard_map/ppermute | solution.py:349
  37.7 0.4 collective-permute-start.9
  38.1 0.3 collective-permute-done.17.refs_19_
  38.4 0.3 collective-permute-start.10
  38.6 5.2 %collective-permute-start.4 = (f32[256,128]{1,0:T(8,128)S(1)}, f32[256,128]{1,0:T(8,128)S(1)}, u32[]{:S(2)}, u32[]{:S(2)}) collective-permute-start(f32[256,128]{1,0:T(8,128)S(1)} %get-tuple-element.46), channel_id=1, source_target_pairs={{0,21},{1,20},{2,23},{3,22},{4,17},{5,16},{6,19},{7,18},{8,29},{9,... | collective-permute-start | bytes 393224 | tf_op jit(solution)/shard_map/ppermute | solution.py:349
  43.9 0.6 collective-permute-start.5
  44.5 4.9 %collective-permute-start.6 = (f32[256,128]{1,0:T(8,128)S(1)}, f32[256,128]{1,0:T(8,128)S(1)}, u32[]{:S(2)}, u32[]{:S(2)}) collective-permute-start(f32[256,128]{1,0:T(8,128)S(1)} %get-tuple-element.48), channel_id=1, source_target_pairs={{0,23},{1,22},{2,21},{3,20},{4,19},{5,18},{6,17},{7,16},{8,31},{9,... | collective-permute-start | bytes 393224 | tf_op jit(solution)/shard_map/ppermute | solution.py:349
  49.4 6.7 %collective-permute-done.4.refs_4_ = f32[256,128]{1,0:T(8,128)S(1)} collective-permute-done((f32[256,128]{1,0:T(8,128)S(1)}, f32[256,128]{1,0:T(8,128)S(1)}, u32[]{:S(2)}, u32[]{:S(2)}) %collective-permute-start.4) | collective-permute-done | bytes 131104 | tf_op jit(solution)/shard_map/ppermute | solution.py:349
  56.1 1.5 %collective-permute-start.11 = (f32[264,128]{1,0:T(8,128)S(1)}, f32[264,128]{1,0:T(8,128)S(1)}, u32[]{:S(2)}, u32[]{:S(2)}) collective-permute-start(f32[264,128]{1,0:T(8,128)S(1)} %get-tuple-element.61), channel_id=1, source_target_pairs={{0,16},{1,17},{2,18},{3,19},{4,20},{5,21},{6,22},{7,23},{8,24},{9,... | collective-permute-start | bytes 405512 | tf_op jit(solution)/shard_map/ppermute | solution.py:349
  57.6 2.2 %collective-permute-start.12 = (f32[264,128]{1,0:T(8,128)S(1)}, f32[264,128]{1,0:T(8,128)S(1)}, u32[]{:S(2)}, u32[]{:S(2)}) collective-permute-start(f32[264,128]{1,0:T(8,128)S(1)} %get-tuple-element.62), channel_id=1, source_target_pairs={{0,3},{1,2},{2,1},{3,0},{4,7},{5,6},{6,5},{7,4},{8,11},{9,10},{10,... | collective-permute-start | bytes 405512 | tf_op jit(solution)/shard_map/ppermute | solution.py:349
  59.8 1.9 %collective-permute-start.13 = (f32[264,128]{1,0:T(8,128)S(1)}, f32[264,128]{1,0:T(8,128)S(1)}, u32[]{:S(2)}, u32[]{:S(2)}) collective-permute-start(f32[264,128]{1,0:T(8,128)S(1)} %get-tuple-element.63), channel_id=1, source_target_pairs={{0,17},{1,16},{2,19},{3,18},{4,21},{5,20},{6,23},{7,22},{8,25},{9,... | collective-permute-start | bytes 405512 | tf_op jit(solution)/shard_map/ppermute | solution.py:349
  61.7 3.2 %collective-permute-start.14 = (f32[264,128]{1,0:T(8,128)S(1)}, f32[264,128]{1,0:T(8,128)S(1)}, u32[]{:S(2)}, u32[]{:S(2)}) collective-permute-start(f32[264,128]{1,0:T(8,128)S(1)} %get-tuple-element.64), channel_id=1, source_target_pairs={{0,18},{1,19},{2,16},{3,17},{4,22},{5,23},{6,20},{7,21},{8,26},{9,... | collective-permute-start | bytes 405512 | tf_op jit(solution)/shard_map/ppermute | solution.py:349
  64.9 3.4 %collective-permute-done.13.refs_11_ = f32[264,128]{1,0:T(8,128)S(1)} collective-permute-done((f32[264,128]{1,0:T(8,128)S(1)}, f32[264,128]{1,0:T(8,128)S(1)}, u32[]{:S(2)}, u32[]{:S(2)}) %collective-permute-start.13) | collective-permute-done | bytes 135200 | tf_op jit(solution)/shard_map/ppermute | solution.py:349
  68.4 1.6 %collective-permute-done.14.refs_12_ = f32[264,128]{1,0:T(8,128)S(1)} collective-permute-done((f32[264,128]{1,0:T(8,128)S(1)}, f32[264,128]{1,0:T(8,128)S(1)}, u32[]{:S(2)}, u32[]{:S(2)}) %collective-permute-start.14) | collective-permute-done | bytes 135200 | tf_op jit(solution)/shard_map/ppermute | solution.py:349
  70.0 2.1 %collective-permute-done.15.refs_13_ = f32[264,128]{1,0:T(8,128)S(1)} collective-permute-done((f32[264,128]{1,0:T(8,128)S(1)}, f32[264,128]{1,0:T(8,128)S(1)}, u32[]{:S(2)}, u32[]{:S(2)}) %collective-permute-start.15) | collective-permute-done | bytes 135200 | tf_op jit(solution)/shard_map/ppermute | solution.py:349
  72.1 2.9 %place.1 = (f32[4096,128]{1,0:T(8,128)}, f32[3]{0:T(128)}) custom-call(bf16[128,256]{1,0:T(8,128)(2,1)S(1)} %copy-done, f32[256,128]{1,0:T(8,128)S(1)} %collective-permute-done.1.refs_1_, f32[256,128]{1,0:T(8,128)S(1)} %collective-permute-done.2.refs_2_, f32[256,128]{1,0:T(8,128)S(1)} %collective-permute-done.3.refs_3_, ...), custom_call_target="tpu_custom_call" | custom-call | tf_op jit(solution)/shard_map/place/pallas_call | solution.py:412
  (18 shorter events, 0.1 us)
Async XLA Ops:
  3.8 68.2 %copy-start = (bf16[128,256]{1,0:T(8,128)(2,1)S(1)}, bf16[128,256]{1,0:T(8,128)(2,1)}, u32[]{:S(2)}) copy-start(bf16[128,256]{1,0:T(8,128)(2,1)} %constant.8.clone.refs_0_) | copy-start | bytes 196612
  3.9 4.3 %collective-permute-start = (f32[1800,128]{1,0:T(8,128)S(1)}, f32[1800,128]{1,0:T(8,128)S(1)}, u32[]{:S(2)}, u32[]{:S(2)}) collective-permute-start(f32[1800,128]{1,0:T(8,128)S(1)} %get-tuple-element.36), channel_id=1, source_target_pairs={{0,8},{1,9},{2,10},{3,11},{4,12},{5,13},{6,14},{7,15},{8,0},{9,1},... | collective-permute-start | bytes 2764808 | tf_op jit(solution)/shard_map/ppermute | solution.py:349
  4.4 11.2 %collective-permute-start.7 = (f32[136,128]{1,0:T(8,128)S(1)}, f32[136,128]{1,0:T(8,128)S(1)}, u32[]{:S(2)}, u32[]{:S(2)}) collective-permute-start(f32[136,128]{1,0:T(8,128)S(1)} %get-tuple-element.50), channel_id=1, source_target_pairs={{0,4},{1,5},{2,6},{3,7},{4,0},{5,1},{6,2},{7,3},{8,12},{9,13},{10,... | collective-permute-start | bytes 208904 | tf_op jit(solution)/shard_map/ppermute | solution.py:349
  8.1 15.4 %collective-permute-start.8 = (f32[136,128]{1,0:T(8,128)S(1)}, f32[136,128]{1,0:T(8,128)S(1)}, u32[]{:S(2)}, u32[]{:S(2)}) collective-permute-start(f32[136,128]{1,0:T(8,128)S(1)} %get-tuple-element.51), channel_id=1, source_target_pairs={{0,12},{1,13},{2,14},{3,15},{4,8},{5,9},{6,10},{7,11},{8,4},{9,5},... | collective-permute-start | bytes 208904 | tf_op jit(solution)/shard_map/ppermute | solution.py:349
  8.1 30.5 %collective-permute-start.1 = (f32[256,128]{1,0:T(8,128)S(1)}, f32[256,128]{1,0:T(8,128)S(1)}, u32[]{:S(2)}, u32[]{:S(2)}) collective-permute-start(f32[256,128]{1,0:T(8,128)S(1)} %get-tuple-element.43), channel_id=1, source_target_pairs={{0,6},{1,7},{2,4},{3,5},{4,2},{5,3},{6,0},{7,1},{8,14},{9,15},{10,... | collective-permute-start | bytes 393224 | tf_op jit(solution)/shard_map/ppermute | solution.py:349
  11.9 32.0 %collective-permute-start.2 = (f32[256,128]{1,0:T(8,128)S(1)}, f32[256,128]{1,0:T(8,128)S(1)}, u32[]{:S(2)}, u32[]{:S(2)}) collective-permute-start(f32[256,128]{1,0:T(8,128)S(1)} %get-tuple-element.44), channel_id=1, source_target_pairs={{0,20},{1,21},{2,22},{3,23},{4,16},{5,17},{6,18},{7,19},{8,28},{9,... | collective-permute-start | bytes 393224 | tf_op jit(solution)/shard_map/ppermute | solution.py:349
  12.2 32.3 %collective-permute-start.3 = (f32[256,128]{1,0:T(8,128)S(1)}, f32[256,128]{1,0:T(8,128)S(1)}, u32[]{:S(2)}, u32[]{:S(2)}) collective-permute-start(f32[256,128]{1,0:T(8,128)S(1)} %get-tuple-element.45), channel_id=1, source_target_pairs={{0,7},{1,6},{2,5},{3,4},{4,3},{5,2},{6,1},{7,0},{8,15},{9,14},{10,... | collective-permute-start | bytes 393224 | tf_op jit(solution)/shard_map/ppermute | solution.py:349
  15.7 22.1 %collective-permute-start.16 = (f32[128,128]{1,0:T(8,128)S(1)}, f32[128,128]{1,0:T(8,128)S(1)}, u32[]{:S(2)}, u32[]{:S(2)}) collective-permute-start(f32[128,128]{1,0:T(8,128)S(1)} %get-tuple-element.66), channel_id=1, source_target_pairs={{0,5},{1,4},{2,7},{3,6},{4,1},{5,0},{6,3},{7,2},{8,13},{9,12},{10,... | collective-permute-start | bytes 196616 | tf_op jit(solution)/shard_map/ppermute | solution.py:349
  23.5 14.9 %collective-permute-start.17 = (f32[128,128]{1,0:T(8,128)S(1)}, f32[128,128]{1,0:T(8,128)S(1)}, u32[]{:S(2)}, u32[]{:S(2)}) collective-permute-start(f32[128,128]{1,0:T(8,128)S(1)} %get-tuple-element.67), channel_id=1, source_target_pairs={{0,13},{1,12},{2,15},{3,14},{4,9},{5,8},{6,11},{7,10},{8,5},{9,4},... | collective-permute-start | bytes 196616 | tf_op jit(solution)/shard_map/ppermute | solution.py:349
  37.7 24.0 %collective-permute-start.9 = (f32[264,128]{1,0:T(8,128)S(1)}, f32[264,128]{1,0:T(8,128)S(1)}, u32[]{:S(2)}, u32[]{:S(2)}) collective-permute-start(f32[264,128]{1,0:T(8,128)S(1)} %get-tuple-element.59), channel_id=1, source_target_pairs={{0,1},{1,0},{2,3},{3,2},{4,5},{5,4},{6,7},{7,6},{8,9},{9,8},{10,11... | collective-permute-start | bytes 405512 | tf_op jit(solution)/shard_map/ppermute | solution.py:349
  38.4 26.5 %collective-permute-start.10 = (f32[264,128]{1,0:T(8,128)S(1)}, f32[264,128]{1,0:T(8,128)S(1)}, u32[]{:S(2)}, u32[]{:S(2)}) collective-permute-start(f32[264,128]{1,0:T(8,128)S(1)} %get-tuple-element.60), channel_id=1, source_target_pairs={{0,2},{1,3},{2,0},{3,1},{4,6},{5,7},{6,4},{7,5},{8,10},{9,11},{10,... | collective-permute-start | bytes 405512 | tf_op jit(solution)/shard_map/ppermute | solution.py:349
  38.6 17.4 %collective-permute-start.4 = (f32[256,128]{1,0:T(8,128)S(1)}, f32[256,128]{1,0:T(8,128)S(1)}, u32[]{:S(2)}, u32[]{:S(2)}) collective-permute-start(f32[256,128]{1,0:T(8,128)S(1)} %get-tuple-element.46), channel_id=1, source_target_pairs={{0,21},{1,20},{2,23},{3,22},{4,17},{5,16},{6,19},{7,18},{8,29},{9,... | collective-permute-start | bytes 393224 | tf_op jit(solution)/shard_map/ppermute | solution.py:349
  43.9 13.7 %collective-permute-start.5 = (f32[256,128]{1,0:T(8,128)S(1)}, f32[256,128]{1,0:T(8,128)S(1)}, u32[]{:S(2)}, u32[]{:S(2)}) collective-permute-start(f32[256,128]{1,0:T(8,128)S(1)} %get-tuple-element.47), channel_id=1, source_target_pairs={{0,22},{1,23},{2,20},{3,21},{4,18},{5,19},{6,16},{7,17},{8,30},{9,... | collective-permute-start | bytes 393224 | tf_op jit(solution)/shard_map/ppermute | solution.py:349
  44.5 15.3 %collective-permute-start.6 = (f32[256,128]{1,0:T(8,128)S(1)}, f32[256,128]{1,0:T(8,128)S(1)}, u32[]{:S(2)}, u32[]{:S(2)}) collective-permute-start(f32[256,128]{1,0:T(8,128)S(1)} %get-tuple-element.48), channel_id=1, source_target_pairs={{0,23},{1,22},{2,21},{3,20},{4,19},{5,18},{6,17},{7,16},{8,31},{9,... | collective-permute-start | bytes 393224 | tf_op jit(solution)/shard_map/ppermute | solution.py:349
  56.1 8.8 %collective-permute-start.11 = (f32[264,128]{1,0:T(8,128)S(1)}, f32[264,128]{1,0:T(8,128)S(1)}, u32[]{:S(2)}, u32[]{:S(2)}) collective-permute-start(f32[264,128]{1,0:T(8,128)S(1)} %get-tuple-element.61), channel_id=1, source_target_pairs={{0,16},{1,17},{2,18},{3,19},{4,20},{5,21},{6,22},{7,23},{8,24},{9,... | collective-permute-start | bytes 405512 | tf_op jit(solution)/shard_map/ppermute | solution.py:349
  57.6 7.3 %collective-permute-start.12 = (f32[264,128]{1,0:T(8,128)S(1)}, f32[264,128]{1,0:T(8,128)S(1)}, u32[]{:S(2)}, u32[]{:S(2)}) collective-permute-start(f32[264,128]{1,0:T(8,128)S(1)} %get-tuple-element.62), channel_id=1, source_target_pairs={{0,3},{1,2},{2,1},{3,0},{4,7},{5,6},{6,5},{7,4},{8,11},{9,10},{10,... | collective-permute-start | bytes 405512 | tf_op jit(solution)/shard_map/ppermute | solution.py:349
  59.8 8.5 %collective-permute-start.13 = (f32[264,128]{1,0:T(8,128)S(1)}, f32[264,128]{1,0:T(8,128)S(1)}, u32[]{:S(2)}, u32[]{:S(2)}) collective-permute-start(f32[264,128]{1,0:T(8,128)S(1)} %get-tuple-element.63), channel_id=1, source_target_pairs={{0,17},{1,16},{2,19},{3,18},{4,21},{5,20},{6,23},{7,22},{8,25},{9,... | collective-permute-start | bytes 405512 | tf_op jit(solution)/shard_map/ppermute | solution.py:349
  61.7 8.2 %collective-permute-start.14 = (f32[264,128]{1,0:T(8,128)S(1)}, f32[264,128]{1,0:T(8,128)S(1)}, u32[]{:S(2)}, u32[]{:S(2)}) collective-permute-start(f32[264,128]{1,0:T(8,128)S(1)} %get-tuple-element.64), channel_id=1, source_target_pairs={{0,18},{1,19},{2,16},{3,17},{4,22},{5,23},{6,20},{7,21},{8,26},{9,... | collective-permute-start | bytes 405512 | tf_op jit(solution)/shard_map/ppermute | solution.py:349
  64.9 7.2 %collective-permute-start.15 = (f32[264,128]{1,0:T(8,128)S(1)}, f32[264,128]{1,0:T(8,128)S(1)}, u32[]{:S(2)}, u32[]{:S(2)}) collective-permute-start(f32[264,128]{1,0:T(8,128)S(1)} %get-tuple-element.65), channel_id=1, source_target_pairs={{0,19},{1,18},{2,17},{3,16},{4,23},{5,22},{6,21},{7,20},{8,27},{9,... | collective-permute-start | bytes 405512 | tf_op jit(solution)/shard_map/ppermute | solution.py:349

commit v3 on v2

--- a/solution.py
+++ b/solution.py
@@ -15,7 +15,7 @@
 RADIX = 2**WINDOW // LANES
 AXES = ("outer", "inner")
 VMEM_LIMIT = 16 * 2**20
-SUB = 32
+SUB = 16
 
 
 def flip(value, count):
@@ -93,7 +93,7 @@
         )
         for block in range(n_devices // 2)
     ]
-    for copy in loads[:1] + [phase_load] + loads[1:2] + table_loads + loads[2:]:
+    for copy in loads[:1] + [phase_load] + loads[1:] + table_loads:
         copy.start()
 
     base = jnp.int32(0)
@@ -132,20 +132,20 @@
                 for residue in range(RADIX):
                     for part in range(2):
                         high, low = halves(folded[residue][part])
-                        where = (residue, pl.ds(row, SUB), pl.ds(part * LANES, LANES))
+                        where = (half, residue, pl.ds(row, SUB), pl.ds(part * LANES, LANES))
                         high_ref[where] = high
                         low_ref[where] = low
             angle = flip(chunk, chunk_bits) * n_devices * angle_scale
             cosine, sine = math.cos(angle), math.sin(angle)
             real_sum += turn_re * cosine + turn_im * sine
             imag_sum += turn_im * cosine - turn_re * sine
-        if half == 0:
-            for copy in table_loads:
-                copy.wait()
+    for copy in table_loads:
+        copy.wait()
+    for half in range(chunks // 2):
         for residue in range(RADIX):
             table_high = table_ref[:, residue].reshape(2 * LANES, 2 * LANES)
             table_low = table_ref[:, RADIX + residue].reshape(2 * LANES, 2 * LANES)
-            high, low = high_ref[residue], low_ref[residue]
+            high, low = high_ref[half, residue], low_ref[half, residue]
             values = dot_rows(table_high, high) + dot_rows(table_high, low)
             values += dot_rows(table_low, high)
             for mask, out, row in targets:
@@ -180,50 +180,55 @@
 
 
 def place_kernel(info, sources, tiles, order_ref, *refs):
-    n_devices, chunks, total_len, device_id = info()
-    ins = refs[:-4]
-    out_ref, checks_ref, held, factor_ref = refs[-4:]
-    group = pl.program_id(0)
+    n_devices, chunks, groups, total_len, device_id = info()
+    ins = refs[:-5]
+    out_hbm, checks_ref, held, out_ref, sems = refs[-5:]
     dev_bits = n_devices.bit_length() - 1
     chunk_bits = chunks.bit_length() - 1
     slot_rows = held.shape[0] // n_devices
 
-    @pl.when(group == 0)
-    def _():
-        turned_id = jnp.int32(0)
-        for bit in range(dev_bits):
-            turned_id += (device_id >> bit & 1) << (dev_bits - 1 - bit)
-        rows = chunks * RADIX * 8
-        for mask, array, offset in sources:
-            slot = turned_id ^ flip(mask, dev_bits)
-            target = pl.ds(pl.multiple_of(slot * slot_rows, 8), rows)
-            held[target, :] = ins[array][pl.ds(offset, rows), :]
-        tile = jnp.zeros((8, LANES), jnp.float32)
-        for array, offset in tiles:
-            tile = tile + ins[array][pl.ds(offset, 8), :]
-        sums = tile.sum(1, keepdims=True)
-        mean_square = jnp.broadcast_to(sums[0:1], (8, LANES)) * (1.0 / total_len)
-        shifted = mean_square + 1e-06
-        factor = lax.rsqrt(shifted)
-        factor = factor * (1.5 - 0.5 * shifted * factor * factor)
-        factor_ref[...] = factor
-        columns = 2**WINDOW
-        scaled = factor * math.sqrt(columns / total_len)
-        checks_ref[0] = mean_square[0, 0]
-        checks_ref[1] = (jnp.broadcast_to(sums[1:2], (8, LANES)) * scaled)[0, 0]
-        checks_ref[2] = (jnp.broadcast_to(sums[2:3], (8, LANES)) * scaled)[0, 0]
-
-    factor = jnp.broadcast_to(factor_ref[0:1], (LANES, LANES))
+    turned_id = jnp.int32(0)
+    for bit in range(dev_bits):
+        turned_id += (device_id >> bit & 1) << (dev_bits - 1 - bit)
+    rows = chunks * RADIX * 8
+    for mask, array, offset in sources:
+        slot = turned_id ^ flip(mask, dev_bits)
+        target = pl.ds(pl.multiple_of(slot * slot_rows, 8), rows)
+        held[target, :] = ins[array][pl.ds(offset, rows), :]
+    tile = jnp.zeros((8, LANES), jnp.float32)
+    for array, offset in tiles:
+        tile = tile + ins[array][pl.ds(offset, 8), :]
+    sums = tile.sum(1, keepdims=True)
+    mean_square = jnp.broadcast_to(sums[0:1], (8, LANES)) * (1.0 / total_len)
+    shifted = mean_square + 1e-06
+    factor = lax.rsqrt(shifted)
+    factor = factor * (1.5 - 0.5 * shifted * factor * factor)
+    columns = 2**WINDOW
+    scaled = factor * math.sqrt(columns / total_len)
+    checks_ref[0] = mean_square[0, 0]
+    checks_ref[1] = (jnp.broadcast_to(sums[1:2], (8, LANES)) * scaled)[0, 0]
+    checks_ref[2] = (jnp.broadcast_to(sums[2:3], (8, LANES)) * scaled)[0, 0]
+
+    factor = jnp.broadcast_to(factor[0:1], (LANES, LANES))
     order = order_ref[...]
-    for residue in range(RADIX):
-        for part in range(2):
-            pieces = []
-            for low in range(chunks):
-                tile_row = (flip(low, chunk_bits) * RADIX + residue) * 8 + part
-                pieces.append(held[pl.ds(tile_row + 2 * group, n_devices, stride=slot_rows), :])
-            high, low = halves(jnp.concatenate(pieces, 0))
-            turned = dot_rows(order, jnp.concatenate([high, low], 1))
-            out_ref[pl.ds(residue * 2 * LANES + part, LANES, stride=2), :] = turned * factor
+    copies = []
+    for group in range(groups):
+        for residue in range(RADIX):
+            for part in range(2):
+                pieces = []
+                for low in range(chunks):
+                    tile_row = (flip(low, chunk_bits) * RADIX + residue) * 8 + 2 * group + part
+                    pieces.append(held[pl.ds(tile_row, n_devices, stride=slot_rows), :])
+                high, low = halves(jnp.concatenate(pieces, 0))
+                turned = dot_rows(order, jnp.concatenate([high, low], 1))
+                row = (group * RADIX + residue) * 2 * LANES + part
+                out_ref[pl.ds(row, LANES, stride=2), :] = turned * factor
+        size = RADIX * 2 * LANES
+        span = pl.ds(group * size, size)
+        copies.append(pltpu.make_async_copy(out_ref.at[span], out_hbm.at[span], sems.at[group]))
+        copies[-1].start()
+    for copy in copies:
+        copy.wait()
 
 
 def reverse_index(values, count):
@@ -342,7 +347,7 @@
         return n_devices, chunks, angle_scale, device_id
 
     def place_info():
-        return n_devices, chunks, total_len, info()[3]
+        return n_devices, chunks, groups, total_len, info()[3]
 
     def exchange(values, mask):
         pairs_of = [(source, source ^ mask) for source in range(n_devices)]
@@ -360,7 +365,6 @@
     tiles = [(stay, rows), (swap, swap_rows), (swap + 1, rows), (swap + 2, rows)]
     constrain = lambda value: pltpu.with_memory_space_constraint(value, pltpu.HBM)
     shaped = lambda count: jax.ShapeDtypeStruct((count, LANES), jnp.float32)
-    whole = lambda shape: pl.BlockSpec(shape, lambda i: (0,) * len(shape))
     hbm = pl.BlockSpec(memory_space=pltpu.HBM)
     vmem = pl.BlockSpec(memory_space=pltpu.VMEM)
     sent = pl.pallas_call(
@@ -372,8 +376,8 @@
             pltpu.VMEM((vectors, LANES), jnp.float32),
             pltpu.VMEM(table.shape[1:], jnp.bfloat16),
             pltpu.VMEM(phase.shape, jnp.float32),
-            pltpu.VMEM((RADIX, 2 * LANES, 2 * LANES), jnp.bfloat16),
-            pltpu.VMEM((RADIX, 2 * LANES, 2 * LANES), jnp.bfloat16),
+            pltpu.VMEM((chunks // 2, RADIX, 2 * LANES, 2 * LANES), jnp.bfloat16),
+            pltpu.VMEM((chunks // 2, RADIX, 2 * LANES, 2 * LANES), jnp.bfloat16),
             pltpu.SemaphoreType.DMA((chunks + 1 + n_devices // 2,)),
         ],
         compiler_params=pltpu.CompilerParams(vmem_limit_bytes=VMEM_LIMIT),
@@ -411,19 +415,16 @@
     sums = tiles + [(len(far) + index, 2 * rows) for index in range(len(near))]
     placed, checks = pl.pallas_call(
         lambda *refs: place_kernel(place_info, sources, sums, *refs),
-        grid=(groups,),
-        in_specs=[whole(order.shape)] + [vmem] * len(arrivals),
-        out_specs=[
-            pl.BlockSpec((vectors // groups, LANES), lambda i: (i, 0)),
-            pl.BlockSpec(memory_space=pltpu.SMEM),
-        ],
+        in_specs=[vmem] * (1 + len(arrivals)),
+        out_specs=[hbm, pl.BlockSpec(memory_space=pltpu.SMEM)],
         out_shape=[
             jax.ShapeDtypeStruct((vectors, LANES), jnp.float32),
             jax.ShapeDtypeStruct((3,), jnp.float32),
         ],
         scratch_shapes=[
             pltpu.VMEM((n_devices * slot_rows, LANES), jnp.float32),
-            pltpu.VMEM((8, LANES), jnp.float32),
+            pltpu.VMEM((vectors, LANES), jnp.float32),
+            pltpu.SemaphoreType.DMA((groups,)),
         ],
         compiler_params=pltpu.CompilerParams(vmem_limit_bytes=VMEM_LIMIT),
         name="place",

time: 75.3 us -> 74.6 us (level)
  no operation moved by 1% of the time
where the time goes in v3:
time: 74.6 us; the launch traced here: 74.3 us
  waiting for transfers between devices  35.2 us (47%)
  starting transfers between devices  33 us (44%)
  Pallas kernels  5.45 us (7%)
    ppermute x18, waiting for transfers between devices, exchange(): return lax.ppermute(values, AXES, pairs_of)  35.2 us
    ppermute x18, starting transfers between devices, exchange(): return lax.ppermute(values, AXES, pairs_of)  33 us
    pallas_call x1, Pallas kernels, per_device(): pl.pallas_call(lambda *refs: transform_kernel(info, targets, tiles, *refs...  3.06 us
    pallas_call x1, Pallas kernels, per_device(): pl.pallas_call(lambda *refs: place_kernel(place_info, sources, sums, *ref...  2.33 us
  transfers between devices with their start and end apart: 18, of which 7 were waited for; matrix products, arithmetic and copies ran while one was open for 0% of the time, Pallas kernels for 0%

profile of v3, /device:TPU:0, one launch (start us, length us, event | category | flops | bytes accessed | tf_op | source)
XLA Modules:
  0.0 74.3 jit_solution(6733371123032699338)
XLA Ops:
  0.6 3.1 %transform.1 = (f32[256,128]{1,0:T(8,128)S(1)}, f32[256,128]{1,0:T(8,128)S(1)}, f32[256,128]{1,0:T(8,128)S(1)}, f32[256,128]{1,0:T(8,128)S(1)}, f32[256,128]{1,0...) custom-call(f32[4096,128]{1,0:T(8,128)} %bitcast.10, ...), custom_call_target="tpu_custom_call" | custom-call | tf_op jit(solution)/shard_map/transform/pallas_call | solution.py:370
  3.7 0.6 collective-permute-start
  4.3 3.7 %collective-permute-start.7 = (f32[136,128]{1,0:T(8,128)S(1)}, f32[136,128]{1,0:T(8,128)S(1)}, u32[]{:S(2)}, u32[]{:S(2)}) collective-permute-start(f32[136,128]{1,0:T(8,128)S(1)} %get-tuple-element.50), channel_id=1, source_target_pairs={{0,4},{1,5},{2,6},{3,7},{4,0},{5,1},{6,2},{7,3},{8,12},{9,13},{10,... | collective-permute-start | bytes 208904 | tf_op jit(solution)/shard_map/ppermute | solution.py:354
  8.0 3.7 %collective-permute-start.1 = (f32[256,128]{1,0:T(8,128)S(1)}, f32[256,128]{1,0:T(8,128)S(1)}, u32[]{:S(2)}, u32[]{:S(2)}) collective-permute-start(f32[256,128]{1,0:T(8,128)S(1)} %get-tuple-element.43), channel_id=1, source_target_pairs={{0,6},{1,7},{2,4},{3,5},{4,2},{5,3},{6,0},{7,1},{8,14},{9,15},{10,... | collective-permute-start | bytes 393224 | tf_op jit(solution)/shard_map/ppermute | solution.py:354
  11.7 0.4 collective-permute-start.2
  12.1 3.4 %collective-permute-start.3 = (f32[256,128]{1,0:T(8,128)S(1)}, f32[256,128]{1,0:T(8,128)S(1)}, u32[]{:S(2)}, u32[]{:S(2)}) collective-permute-start(f32[256,128]{1,0:T(8,128)S(1)} %get-tuple-element.45), channel_id=1, source_target_pairs={{0,7},{1,6},{2,5},{3,4},{4,3},{5,2},{6,1},{7,0},{8,15},{9,14},{10,... | collective-permute-start | bytes 393224 | tf_op jit(solution)/shard_map/ppermute | solution.py:354
  15.5 1.0 %collective-permute-start.16 = (f32[128,128]{1,0:T(8,128)S(1)}, f32[128,128]{1,0:T(8,128)S(1)}, u32[]{:S(2)}, u32[]{:S(2)}) collective-permute-start(f32[128,128]{1,0:T(8,128)S(1)} %get-tuple-element.66), channel_id=1, source_target_pairs={{0,5},{1,4},{2,7},{3,6},{4,1},{5,0},{6,3},{7,2},{8,13},{9,12},{10,... | collective-permute-start | bytes 196616 | tf_op jit(solution)/shard_map/ppermute | solution.py:354
  16.5 6.8 %collective-permute-done.8.refs_3_.refs_17_ = f32[136,128]{1,0:T(8,128)S(1)} collective-permute-done((f32[136,128]{1,0:T(8,128)S(1)}, f32[136,128]{1,0:T(8,128)S(1)}, u32[]{:S(2)}, u32[]{:S(2)}) %collective-permute-start.8) | collective-permute-done | bytes 69664 | tf_op jit(solution)/shard_map/ppermute | solution.py:354
  23.4 14.2 %collective-permute-done.16.refs_18_ = f32[128,128]{1,0:T(8,128)S(1)} collective-permute-done((f32[128,128]{1,0:T(8,128)S(1)}, f32[128,128]{1,0:T(8,128)S(1)}, u32[]{:S(2)}, u32[]{:S(2)}) %collective-permute-start.16) | collective-permute-done | bytes 65568 | tf_op jit(solution)/shard_map/ppermute | solution.py:354
  37.6 0.4 collective-permute-start.9
  38.0 0.3 collective-permute-done.17.refs_19_
  38.2 0.3 collective-permute-start.10
  38.5 5.2 %collective-permute-start.4 = (f32[256,128]{1,0:T(8,128)S(1)}, f32[256,128]{1,0:T(8,128)S(1)}, u32[]{:S(2)}, u32[]{:S(2)}) collective-permute-start(f32[256,128]{1,0:T(8,128)S(1)} %get-tuple-element.46), channel_id=1, source_target_pairs={{0,21},{1,20},{2,23},{3,22},{4,17},{5,16},{6,19},{7,18},{8,29},{9,... | collective-permute-start | bytes 393224 | tf_op jit(solution)/shard_map/ppermute | solution.py:354
  43.7 0.6 collective-permute-start.5
  44.4 4.9 %collective-permute-start.6 = (f32[256,128]{1,0:T(8,128)S(1)}, f32[256,128]{1,0:T(8,128)S(1)}, u32[]{:S(2)}, u32[]{:S(2)}) collective-permute-start(f32[256,128]{1,0:T(8,128)S(1)} %get-tuple-element.48), channel_id=1, source_target_pairs={{0,23},{1,22},{2,21},{3,20},{4,19},{5,18},{6,17},{7,16},{8,31},{9,... | collective-permute-start | bytes 393224 | tf_op jit(solution)/shard_map/ppermute | solution.py:354
  49.2 6.7 %collective-permute-done.4.refs_4_ = f32[256,128]{1,0:T(8,128)S(1)} collective-permute-done((f32[256,128]{1,0:T(8,128)S(1)}, f32[256,128]{1,0:T(8,128)S(1)}, u32[]{:S(2)}, u32[]{:S(2)}) %collective-permute-start.4) | collective-permute-done | bytes 131104 | tf_op jit(solution)/shard_map/ppermute | solution.py:354
  55.9 1.5 %collective-permute-start.11 = (f32[264,128]{1,0:T(8,128)S(1)}, f32[264,128]{1,0:T(8,128)S(1)}, u32[]{:S(2)}, u32[]{:S(2)}) collective-permute-start(f32[264,128]{1,0:T(8,128)S(1)} %get-tuple-element.61), channel_id=1, source_target_pairs={{0,16},{1,17},{2,18},{3,19},{4,20},{5,21},{6,22},{7,23},{8,24},{9,... | collective-permute-start | bytes 405512 | tf_op jit(solution)/shard_map/ppermute | solution.py:354
  57.5 2.2 %collective-permute-start.12 = (f32[264,128]{1,0:T(8,128)S(1)}, f32[264,128]{1,0:T(8,128)S(1)}, u32[]{:S(2)}, u32[]{:S(2)}) collective-permute-start(f32[264,128]{1,0:T(8,128)S(1)} %get-tuple-element.62), channel_id=1, source_target_pairs={{0,3},{1,2},{2,1},{3,0},{4,7},{5,6},{6,5},{7,4},{8,11},{9,10},{10,... | collective-permute-start | bytes 405512 | tf_op jit(solution)/shard_map/ppermute | solution.py:354
  59.7 1.9 %collective-permute-start.13 = (f32[264,128]{1,0:T(8,128)S(1)}, f32[264,128]{1,0:T(8,128)S(1)}, u32[]{:S(2)}, u32[]{:S(2)}) collective-permute-start(f32[264,128]{1,0:T(8,128)S(1)} %get-tuple-element.63), channel_id=1, source_target_pairs={{0,17},{1,16},{2,19},{3,18},{4,21},{5,20},{6,23},{7,22},{8,25},{9,... | collective-permute-start | bytes 405512 | tf_op jit(solution)/shard_map/ppermute | solution.py:354
  61.6 3.2 %collective-permute-start.14 = (f32[264,128]{1,0:T(8,128)S(1)}, f32[264,128]{1,0:T(8,128)S(1)}, u32[]{:S(2)}, u32[]{:S(2)}) collective-permute-start(f32[264,128]{1,0:T(8,128)S(1)} %get-tuple-element.64), channel_id=1, source_target_pairs={{0,18},{1,19},{2,16},{3,17},{4,22},{5,23},{6,20},{7,21},{8,26},{9,... | collective-permute-start | bytes 405512 | tf_op jit(solution)/shard_map/ppermute | solution.py:354
  64.8 3.4 %collective-permute-done.13.refs_11_ = f32[264,128]{1,0:T(8,128)S(1)} collective-permute-done((f32[264,128]{1,0:T(8,128)S(1)}, f32[264,128]{1,0:T(8,128)S(1)}, u32[]{:S(2)}, u32[]{:S(2)}) %collective-permute-start.13) | collective-permute-done | bytes 135200 | tf_op jit(solution)/shard_map/ppermute | solution.py:354
  68.3 1.6 %collective-permute-done.14.refs_12_ = f32[264,128]{1,0:T(8,128)S(1)} collective-permute-done((f32[264,128]{1,0:T(8,128)S(1)}, f32[264,128]{1,0:T(8,128)S(1)}, u32[]{:S(2)}, u32[]{:S(2)}) %collective-permute-start.14) | collective-permute-done | bytes 135200 | tf_op jit(solution)/shard_map/ppermute | solution.py:354
  69.8 2.1 %collective-permute-done.15.refs_13_ = f32[264,128]{1,0:T(8,128)S(1)} collective-permute-done((f32[264,128]{1,0:T(8,128)S(1)}, f32[264,128]{1,0:T(8,128)S(1)}, u32[]{:S(2)}, u32[]{:S(2)}) %collective-permute-start.15) | collective-permute-done | bytes 135200 | tf_op jit(solution)/shard_map/ppermute | solution.py:354
  71.9 2.3 %place.1 = (f32[4096,128]{1,0:T(8,128)}, f32[3]{0:T(128)}) custom-call(bf16[128,256]{1,0:T(8,128)(2,1)S(1)} %copy-done, f32[256,128]{1,0:T(8,128)S(1)} %collective-permute-done.1.refs_1_, f32[256,128]{1,0:T(8,128)S(1)} %collective-permute-done.2.refs_2_, f32[256,128]{1,0:T(8,128)S(1)} %collective-permute-done.3.refs_3_, ...), custom_call_target="tpu_custom_call" | custom-call | tf_op jit(solution)/shard_map/place/pallas_call | solution.py:416
  (18 shorter events, 0.1 us)
Async XLA Ops:
  3.7 68.3 %copy-start = (bf16[128,256]{1,0:T(8,128)(2,1)S(1)}, bf16[128,256]{1,0:T(8,128)(2,1)}, u32[]{:S(2)}) copy-start(bf16[128,256]{1,0:T(8,128)(2,1)} %constant.8.clone.refs_0_) | copy-start | bytes 196612
  3.7 4.3 %collective-permute-start = (f32[1800,128]{1,0:T(8,128)S(1)}, f32[1800,128]{1,0:T(8,128)S(1)}, u32[]{:S(2)}, u32[]{:S(2)}) collective-permute-start(f32[1800,128]{1,0:T(8,128)S(1)} %get-tuple-element.36), channel_id=1, source_target_pairs={{0,8},{1,9},{2,10},{3,11},{4,12},{5,13},{6,14},{7,15},{8,0},{9,1},... | collective-permute-start | bytes 2764808 | tf_op jit(solution)/shard_map/ppermute | solution.py:354
  4.3 11.2 %collective-permute-start.7 = (f32[136,128]{1,0:T(8,128)S(1)}, f32[136,128]{1,0:T(8,128)S(1)}, u32[]{:S(2)}, u32[]{:S(2)}) collective-permute-start(f32[136,128]{1,0:T(8,128)S(1)} %get-tuple-element.50), channel_id=1, source_target_pairs={{0,4},{1,5},{2,6},{3,7},{4,0},{5,1},{6,2},{7,3},{8,12},{9,13},{10,... | collective-permute-start | bytes 208904 | tf_op jit(solution)/shard_map/ppermute | solution.py:354
  7.9 15.4 %collective-permute-start.8 = (f32[136,128]{1,0:T(8,128)S(1)}, f32[136,128]{1,0:T(8,128)S(1)}, u32[]{:S(2)}, u32[]{:S(2)}) collective-permute-start(f32[136,128]{1,0:T(8,128)S(1)} %get-tuple-element.51), channel_id=1, source_target_pairs={{0,12},{1,13},{2,14},{3,15},{4,8},{5,9},{6,10},{7,11},{8,4},{9,5},... | collective-permute-start | bytes 208904 | tf_op jit(solution)/shard_map/ppermute | solution.py:354
  8.0 30.5 %collective-permute-start.1 = (f32[256,128]{1,0:T(8,128)S(1)}, f32[256,128]{1,0:T(8,128)S(1)}, u32[]{:S(2)}, u32[]{:S(2)}) collective-permute-start(f32[256,128]{1,0:T(8,128)S(1)} %get-tuple-element.43), channel_id=1, source_target_pairs={{0,6},{1,7},{2,4},{3,5},{4,2},{5,3},{6,0},{7,1},{8,14},{9,15},{10,... | collective-permute-start | bytes 393224 | tf_op jit(solution)/shard_map/ppermute | solution.py:354
  11.7 32.0 %collective-permute-start.2 = (f32[256,128]{1,0:T(8,128)S(1)}, f32[256,128]{1,0:T(8,128)S(1)}, u32[]{:S(2)}, u32[]{:S(2)}) collective-permute-start(f32[256,128]{1,0:T(8,128)S(1)} %get-tuple-element.44), channel_id=1, source_target_pairs={{0,20},{1,21},{2,22},{3,23},{4,16},{5,17},{6,18},{7,19},{8,28},{9,... | collective-permute-start | bytes 393224 | tf_op jit(solution)/shard_map/ppermute | solution.py:354
  12.1 32.3 %collective-permute-start.3 = (f32[256,128]{1,0:T(8,128)S(1)}, f32[256,128]{1,0:T(8,128)S(1)}, u32[]{:S(2)}, u32[]{:S(2)}) collective-permute-start(f32[256,128]{1,0:T(8,128)S(1)} %get-tuple-element.45), channel_id=1, source_target_pairs={{0,7},{1,6},{2,5},{3,4},{4,3},{5,2},{6,1},{7,0},{8,15},{9,14},{10,... | collective-permute-start | bytes 393224 | tf_op jit(solution)/shard_map/ppermute | solution.py:354
  15.5 22.1 %collective-permute-start.16 = (f32[128,128]{1,0:T(8,128)S(1)}, f32[128,128]{1,0:T(8,128)S(1)}, u32[]{:S(2)}, u32[]{:S(2)}) collective-permute-start(f32[128,128]{1,0:T(8,128)S(1)} %get-tuple-element.66), channel_id=1, source_target_pairs={{0,5},{1,4},{2,7},{3,6},{4,1},{5,0},{6,3},{7,2},{8,13},{9,12},{10,... | collective-permute-start | bytes 196616 | tf_op jit(solution)/shard_map/ppermute | solution.py:354
  23.3 14.9 %collective-permute-start.17 = (f32[128,128]{1,0:T(8,128)S(1)}, f32[128,128]{1,0:T(8,128)S(1)}, u32[]{:S(2)}, u32[]{:S(2)}) collective-permute-start(f32[128,128]{1,0:T(8,128)S(1)} %get-tuple-element.67), channel_id=1, source_target_pairs={{0,13},{1,12},{2,15},{3,14},{4,9},{5,8},{6,11},{7,10},{8,5},{9,4},... | collective-permute-start | bytes 196616 | tf_op jit(solution)/shard_map/ppermute | solution.py:354
  37.6 24.0 %collective-permute-start.9 = (f32[264,128]{1,0:T(8,128)S(1)}, f32[264,128]{1,0:T(8,128)S(1)}, u32[]{:S(2)}, u32[]{:S(2)}) collective-permute-start(f32[264,128]{1,0:T(8,128)S(1)} %get-tuple-element.59), channel_id=1, source_target_pairs={{0,1},{1,0},{2,3},{3,2},{4,5},{5,4},{6,7},{7,6},{8,9},{9,8},{10,11... | collective-permute-start | bytes 405512 | tf_op jit(solution)/shard_map/ppermute | solution.py:354
  38.2 26.6 %collective-permute-start.10 = (f32[264,128]{1,0:T(8,128)S(1)}, f32[264,128]{1,0:T(8,128)S(1)}, u32[]{:S(2)}, u32[]{:S(2)}) collective-permute-start(f32[264,128]{1,0:T(8,128)S(1)} %get-tuple-element.60), channel_id=1, source_target_pairs={{0,2},{1,3},{2,0},{3,1},{4,6},{5,7},{6,4},{7,5},{8,10},{9,11},{10,... | collective-permute-start | bytes 405512 | tf_op jit(solution)/shard_map/ppermute | solution.py:354
  38.5 17.4 %collective-permute-start.4 = (f32[256,128]{1,0:T(8,128)S(1)}, f32[256,128]{1,0:T(8,128)S(1)}, u32[]{:S(2)}, u32[]{:S(2)}) collective-permute-start(f32[256,128]{1,0:T(8,128)S(1)} %get-tuple-element.46), channel_id=1, source_target_pairs={{0,21},{1,20},{2,23},{3,22},{4,17},{5,16},{6,19},{7,18},{8,29},{9,... | collective-permute-start | bytes 393224 | tf_op jit(solution)/shard_map/ppermute | solution.py:354
  43.7 13.7 %collective-permute-start.5 = (f32[256,128]{1,0:T(8,128)S(1)}, f32[256,128]{1,0:T(8,128)S(1)}, u32[]{:S(2)}, u32[]{:S(2)}) collective-permute-start(f32[256,128]{1,0:T(8,128)S(1)} %get-tuple-element.47), channel_id=1, source_target_pairs={{0,22},{1,23},{2,20},{3,21},{4,18},{5,19},{6,16},{7,17},{8,30},{9,... | collective-permute-start | bytes 393224 | tf_op jit(solution)/shard_map/ppermute | solution.py:354
  44.4 15.3 %collective-permute-start.6 = (f32[256,128]{1,0:T(8,128)S(1)}, f32[256,128]{1,0:T(8,128)S(1)}, u32[]{:S(2)}, u32[]{:S(2)}) collective-permute-start(f32[256,128]{1,0:T(8,128)S(1)} %get-tuple-element.48), channel_id=1, source_target_pairs={{0,23},{1,22},{2,21},{3,20},{4,19},{5,18},{6,17},{7,16},{8,31},{9,... | collective-permute-start | bytes 393224 | tf_op jit(solution)/shard_map/ppermute | solution.py:354
  55.9 8.9 %collective-permute-start.11 = (f32[264,128]{1,0:T(8,128)S(1)}, f32[264,128]{1,0:T(8,128)S(1)}, u32[]{:S(2)}, u32[]{:S(2)}) collective-permute-start(f32[264,128]{1,0:T(8,128)S(1)} %get-tuple-element.61), channel_id=1, source_target_pairs={{0,16},{1,17},{2,18},{3,19},{4,20},{5,21},{6,22},{7,23},{8,24},{9,... | collective-permute-start | bytes 405512 | tf_op jit(solution)/shard_map/ppermute | solution.py:354
  57.5 7.3 %collective-permute-start.12 = (f32[264,128]{1,0:T(8,128)S(1)}, f32[264,128]{1,0:T(8,128)S(1)}, u32[]{:S(2)}, u32[]{:S(2)}) collective-permute-start(f32[264,128]{1,0:T(8,128)S(1)} %get-tuple-element.62), channel_id=1, source_target_pairs={{0,3},{1,2},{2,1},{3,0},{4,7},{5,6},{6,5},{7,4},{8,11},{9,10},{10,... | collective-permute-start | bytes 405512 | tf_op jit(solution)/shard_map/ppermute | solution.py:354
  59.7 8.6 %collective-permute-start.13 = (f32[264,128]{1,0:T(8,128)S(1)}, f32[264,128]{1,0:T(8,128)S(1)}, u32[]{:S(2)}, u32[]{:S(2)}) collective-permute-start(f32[264,128]{1,0:T(8,128)S(1)} %get-tuple-element.63), channel_id=1, source_target_pairs={{0,17},{1,16},{2,19},{3,18},{4,21},{5,20},{6,23},{7,22},{8,25},{9,... | collective-permute-start | bytes 405512 | tf_op jit(solution)/shard_map/ppermute | solution.py:354
  61.6 8.2 %collective-permute-start.14 = (f32[264,128]{1,0:T(8,128)S(1)}, f32[264,128]{1,0:T(8,128)S(1)}, u32[]{:S(2)}, u32[]{:S(2)}) collective-permute-start(f32[264,128]{1,0:T(8,128)S(1)} %get-tuple-element.64), channel_id=1, source_target_pairs={{0,18},{1,19},{2,16},{3,17},{4,22},{5,23},{6,20},{7,21},{8,26},{9,... | collective-permute-start | bytes 405512 | tf_op jit(solution)/shard_map/ppermute | solution.py:354
  64.8 7.2 %collective-permute-start.15 = (f32[264,128]{1,0:T(8,128)S(1)}, f32[264,128]{1,0:T(8,128)S(1)}, u32[]{:S(2)}, u32[]{:S(2)}) collective-permute-start(f32[264,128]{1,0:T(8,128)S(1)} %get-tuple-element.65), channel_id=1, source_target_pairs={{0,19},{1,18},{2,17},{3,16},{4,23},{5,22},{6,21},{7,20},{8,27},{9,... | collective-permute-start | bytes 405512 | tf_op jit(solution)/shard_map/ppermute | solution.py:354
